TPU v7x, 256 devices: a 8x8x2 block of a 8x8x16 slice. The times are simulated.
256 devices in a mesh: img: 2 (over z), ga: 16 (over y, core), band: 8 (over x).
Axes of the slice: x: 8, y: 8, z: 2, core: 2. Of those that a mesh axis runs over, the one named last changes fastest.
The devices are a block of a 8x8x16 slice.
Arguments:
- orbitals: bfloat16 [1536, 49152], P(('img', 'band'), 'ga'), parts along dimension 0, as said below
- kernel: float32 [49152], P('ga'), may hold values from 0.3 to 3
- block_vectors: bfloat16 [512, 49152], P(('img', 'band'), 'ga'), parts along dimension 0
Outputs:
- ace_vectors: bfloat16 [1536, 49152], P(('img', 'band'), 'ga'), parts along dimension 0
- exchange_block: bfloat16 [512, 49152], P(('img', 'band'), 'ga'), parts along dimension 0
There are 2 independent parts, one for each index of `img`. A program takes and returns all parts, laid end to end along the dimension named above; an argument that names none is the same for every part. Nothing has to cross between parts.
Inputs may be any that keep to these rules, and one draw needn't show every extreme that they name: `orbitals`: the bands of one image are linearly independent, and the block lies largely in their span.
All inputs are finite; a program needn't handle non-finite values.
Results may differ from a plain program's by a relative error of at most 0.02.
Values may be sent and summed in bfloat16 or wider, within the bound.
No kernel may reach another device: no remote copies, remote signals or barrier semaphores. Data moves between devices by JAX's collectives and lax.ppermute only.
A program may use at most 64 MiB of HBM per device.

v0:
```python
import jax
import jax.numpy as jnp
from jax import lax
from jax.sharding import PartitionSpec as P


def over_pieces(shard, axis):
    pieces = lax.all_gather(shard, axis).astype(jnp.float32)
    return pieces.sum(axis=0)


def from_everyone(shard, axis):
    count = lax.axis_size(axis)
    return lax.all_to_all(
        jnp.broadcast_to(shard[None], (count, *shard.shape)), axis, 0, 0, tiled=True
    )


def in_order(pieces, dim):
    pieces = jnp.moveaxis(pieces, 0, dim)
    dims = pieces.shape
    return pieces.reshape(*dims[:dim], dims[dim] * dims[dim + 1], *dims[dim + 2 :])


def gathered_copies(shard, axis, dim):
    pieces = from_everyone(shard, axis)
    return in_order(pieces, dim)


def taken_together(shard, axis):
    return from_everyone(shard, axis).astype(jnp.float32).sum(axis=0)


def cut_along(shard, dim, count):
    dims = shard.shape
    pieces = shard.reshape(*dims[:dim], count, dims[dim] // count, *dims[dim + 1 :])
    return jnp.moveaxis(pieces, dim, 0)


def sent_and_summed(shard, axis, dim):
    pieces = cut_along(shard, dim, lax.axis_size(axis))
    arrived = lax.all_to_all(pieces, axis, split_axis=0, concat_axis=0, tiled=True)
    return arrived.astype(jnp.float32).sum(axis=0)


def contract_first(left, right):
    return lax.dot_general(left, right, (((0,), (0,)), ((), ())), precision=lax.Precision.HIGHEST)


def shards(orbitals, kernel, block_vectors):
    groups = lax.axis_size("ga")
    own_band = lax.axis_index("band")
    total_coeffs = orbitals.shape[1] * groups
    full_orbitals, full_block = (
        lax.all_gather(orbitals, "band", axis=0, tiled=True),
        lax.all_gather(block_vectors, "band", axis=0, tiled=True),
    )
    weighted = (-(full_orbitals.astype(jnp.float32) * kernel[None, :])).astype(jnp.bfloat16)
    own_rows = orbitals.shape[0]
    partial_rows = lax.dot_general(
        orbitals, weighted, (((1,), (1,)), ((), ())), preferred_element_type=jnp.float32
    )
    summed_rows = over_pieces(partial_rows.astype(jnp.bfloat16), "ga").astype(jnp.float32)
    margin = (
        -gathered_copies(summed_rows.astype(jnp.bfloat16), "band", 0).astype(summed_rows.dtype)
        / total_coeffs
    )
    factor = jnp.linalg.cholesky(margin)
    identity = jnp.eye(factor.shape[0], dtype=jnp.float32)
    inverse = lax.linalg.triangular_solve(factor, identity, left_side=True, lower=True)
    inverse_rows = lax.dynamic_slice_in_dim(inverse, own_band * own_rows, own_rows, 0)
    projector = jnp.dot(inverse_rows, weighted.astype(jnp.float32), precision=lax.Precision.HIGHEST)
    local_coupling = jnp.dot(
        projector, full_block.astype(jnp.float32).T, precision=lax.Precision.HIGHEST
    )
    coupling = (
        taken_together(local_coupling.astype(jnp.bfloat16), "ga").astype(jnp.float32) / total_coeffs
    )
    applied = sent_and_summed(
        (-contract_first(coupling, projector)).astype(jnp.bfloat16), "band", 0
    )
    return (projector.astype(jnp.bfloat16), applied.astype(jnp.bfloat16))


def solution(mesh):
    placed = (P(("img", "band"), "ga"), P("ga"), P(("img", "band"), "ga"))
    return jax.shard_map(
        shards,
        mesh=mesh,
        in_specs=placed,
        out_specs=(P(("img", "band"), "ga"), P(("img", "band"), "ga")),
        check_vma=False,
    )
```

profile of v0, /device:TPU:513, one launch (start us, length us, event | category | flops | bytes accessed | tf_op | source)
XLA Modules:
  0.0 510.5 jit_solution(14080767505893318742)
XLA Ops:
  7.2 0.7 all-gather.5.cloned.1.call-update
  8.0 80.9 %all-gather.5.cloned.1.call-done = bf16[768,3072]{1,0:T(8,128)(2,1)} async-done(((bf16[96,3072]{1,0:T(8,128)(2,1)}), bf16[768,3072]{1,0:T(8,128)(2,1)}) %all-gather.5.cloned.1.call-update) | async-done | bytes 4718608 | tf_op jit(solution)/shard_map/all_gather | solution.py:55
  89.0 4.7 fusion.21
  93.8 41.2 %all-gather.9.cloned.1.call-done = bf16[1536,768]{1,0:T(8,128)(2,1)} async-done(((bf16[96,768]{1,0:T(8,128)(2,1)}), bf16[1536,768]{1,0:T(8,128)(2,1)}) %all-gather.9.cloned.1.call-update) | async-done | bytes 2359312 | tf_op jit(solution)/shard_map/all_gather | solution.py:8
  134.9 2.0 reduce_sum.33
  136.9 1.1 broadcast_in_dim.5
  138.0 6.4 %all-to-all-start = ((bf16[8,96,768]{2,1,0:T(8,128)(2,1)}), bf16[8,96,768]{2,1,0:T(8,128)(2,1)S(1)}, u32[]{:S(2)}, u32[]{:S(2)}) async-start(bf16[8,96,768]{2,1,0:T(8,128)(2,1)} %broadcast_in_dim.5), calls=%async_computation | async-start | bytes 2359296 | tf_op jit(solution)/shard_map/all_to_all | solution.py:14
  144.5 0.7 all-gather.7.cloned.1.call-update
  145.3 1.0 iota_compare_fusion
  146.3 1.6 fusion.25
  147.9 35.2 %all-to-all-done = bf16[8,96,768]{2,1,0:T(8,128)(2,1)S(1)} async-done(((bf16[8,96,768]{2,1,0:T(8,128)(2,1)}), bf16[8,96,768]{2,1,0:T(8,128)(2,1)S(1)}, u32[]{:S(2)}, u32[]{:S(2)}) %all-to-all-start) | async-done | bytes 1179680 | tf_op jit(solution)/shard_map/all_to_all | solution.py:14
  183.3 2.6 copy.7
  185.8 1.9 fusion.3
  187.8 1.5 copy-done.1
  189.2 11.7 %cholesky.165 = f32[128,128]{1,0:T(8,128)S(1)} custom-call(f32[128,128]{1,0:T(8,128)S(1)} %cholesky.424), custom_call_target="Cholesky" | custom-call | tf_op jit(solution)/shard_map/jit(cholesky)/cholesky | solution.py:68
  201.0 9.8 %custom-call.46 = f32[1,128,128]{1,2,0:T(8,128)S(1)} custom-call(f32[1,128,128]{2,1,0:T(8,128)S(1)} %get-tuple-element.45), custom_call_target="InvertDiagBlocksLowerTriangular" | custom-call | tf_op jit(solution)/shard_map/jit(cholesky)/cholesky | solution.py:68
  211.0 1.4 constant_dynamic-update-slice_fusion.15
  212.3 1.4 convolution_subtract_fusion.4
  213.8 11.7 %cholesky.188 = f32[128,128]{1,0:T(8,128)S(1)} custom-call(f32[128,128]{1,0:T(8,128)S(1)} %cholesky.428), custom_call_target="Cholesky" | custom-call | tf_op jit(solution)/shard_map/jit(cholesky)/cholesky | solution.py:68
  225.5 10.0 %custom-call.47 = f32[1,128,128]{1,2,0:T(8,128)S(1)} custom-call(f32[1,128,128]{2,1,0:T(8,128)S(1)} %get-tuple-element.42), custom_call_target="InvertDiagBlocksLowerTriangular" | custom-call | tf_op jit(solution)/shard_map/jit(cholesky)/cholesky | solution.py:68
  235.9 1.5 convolution_subtract_fusion.5
  237.4 11.7 %cholesky.354 = f32[128,128]{1,0:T(8,128)S(1)} custom-call(f32[128,128]{1,0:T(8,128)S(1)} %cholesky.433), custom_call_target="Cholesky" | custom-call | tf_op jit(solution)/shard_map/jit(cholesky)/cholesky | solution.py:68
  249.2 0.7 compare_reduce_fusion.3
  249.9 9.8 %custom-call.48 = f32[1,128,128]{1,2,0:T(8,128)S(1)} custom-call(f32[1,128,128]{2,1,0:T(8,128)S(1)} %get-tuple-element.39), custom_call_target="InvertDiagBlocksLowerTriangular" | custom-call | tf_op jit(solution)/shard_map/jit(cholesky)/cholesky | solution.py:68
  260.0 1.6 convolution_subtract_fusion.6
  261.6 12.1 %cholesky.373 = f32[128,128]{1,0:T(8,128)S(1)} custom-call(f32[128,128]{1,0:T(8,128)S(1)} %cholesky.438), custom_call_target="Cholesky" | custom-call | tf_op jit(solution)/shard_map/jit(cholesky)/cholesky | solution.py:68
  273.7 0.7 compare_reduce_fusion.2
  274.4 9.8 %custom-call.49 = f32[1,128,128]{1,2,0:T(8,128)S(1)} custom-call(f32[1,128,128]{2,1,0:T(8,128)S(1)} %get-tuple-element.36), custom_call_target="InvertDiagBlocksLowerTriangular" | custom-call | tf_op jit(solution)/shard_map/jit(cholesky)/cholesky | solution.py:68
  284.5 1.5 convolution_subtract_fusion.7
  286.0 11.7 %cholesky.392 = f32[128,128]{1,0:T(8,128)S(1)} custom-call(f32[128,128]{1,0:T(8,128)S(1)} %cholesky.443), custom_call_target="Cholesky" | custom-call | tf_op jit(solution)/shard_map/jit(cholesky)/cholesky | solution.py:68
  297.7 0.7 compare_reduce_fusion.1
  298.4 9.8 %custom-call.50 = f32[1,128,128]{1,2,0:T(8,128)S(1)} custom-call(f32[1,128,128]{2,1,0:T(8,128)S(1)} %get-tuple-element.33), custom_call_target="InvertDiagBlocksLowerTriangular" | custom-call | tf_op jit(solution)/shard_map/jit(cholesky)/cholesky | solution.py:68
  308.4 1.3 convolution_subtract_fusion.8
  309.8 11.9 %cholesky.410 = f32[128,128]{1,0:T(8,128)S(1)} custom-call(f32[128,128]{1,0:T(8,128)S(1)} %convolution_subtract_fusion.8), custom_call_target="Cholesky" | custom-call | tf_op jit(solution)/shard_map/jit(cholesky)/cholesky | solution.py:68
  321.7 0.7 compare_reduce_fusion
  322.3 0.7 compare_reduce_fusion.4
  326.8 1.6 select_select_fusion
  328.4 21.5 %while.1 = (s32[]{:T(128)}, f32[768,768]{1,0:T(8,128)}, s32[6,2]{0,1:T(2,128)S(1)}, f32[6,128,128]{2,1,0:T(8,128)}, s32[]{:T(128)}) while((s32[]{:T(128)}, f32[768,768]{1,0:T(8,128)}, s32[6,2]{0,1:T(2,128)S(1)}, f32[6,128,128]{2,1,0:T(8,128)}, s32[]{:T(128)}) %tuple.45), condition=%wide.while_cond, body=%wide.while_body.sunk | while | flops 2 | bytes 132705 | solution.py:70
  328.5 0.6 fusion.79
  329.1 2.9 bitcast_dynamic-update-slice_fusion.2
  332.1 0.6 fusion.79
  332.7 2.9 bitcast_dynamic-update-slice_fusion.2
  335.7 0.6 fusion.79
  336.3 2.9 bitcast_dynamic-update-slice_fusion.2
  339.3 0.6 fusion.79
  339.9 2.9 bitcast_dynamic-update-slice_fusion.2
  342.9 0.6 fusion.79
  343.5 2.9 bitcast_dynamic-update-slice_fusion.2
  346.5 0.6 fusion.79
  347.1 2.8 bitcast_dynamic-update-slice_fusion.2
  349.9 59.8 %custom-call.51 = f32[6,128,128]{1,2,0:T(8,128)S(1)} custom-call(f32[6,128,128]{2,1,0:T(8,128)} %get-tuple-element.9), custom_call_target="InvertDiagBlocksLowerTriangular" | custom-call | tf_op jit(solution)/shard_map/triangular_solve | solution.py:70
  409.7 1.2 constant_dynamic-update-slice_fusion.4
  410.9 1.5 convolution_subtract_fusion.2
  412.4 0.5 constant_dynamic-update-slice_fusion.3
  412.9 1.5 convolution_subtract_fusion.3
  415.0 2.0 convolution_subtract_fusion.1
  417.5 2.0 fusion.12
  420.0 2.3 convolution_subtract_fusion
  422.9 3.7 fusion.65
  426.6 3.0 convolution_convert_fusion
  429.7 27.3 %all_to_all.15 = bf16[16,96,256]{2,1,0:T(8,128)(2,1)S(1)} all-to-all(bf16[16,96,256]{2,1,0:T(8,128)(2,1)S(1)} %broadcast_in_dim.7), channel_id=1, replica_groups=mesh['img'=2,'ga'=16,'band'=8] {'ga'}, dimensions={0} | all-to-all | bytes 1572864 | tf_op jit(solution)/shard_map/all_to_all | solution.py:14
  457.1 2.7 fusion
  459.9 43.0 %all_to_all.16 = bf16[8,32,3072]{2,1,0:T(8,128)(2,1)S(1)} all-to-all(bf16[8,32,3072]{2,1,0:T(8,128)(2,1)S(1)} %bitcast.88), channel_id=1, replica_groups=mesh['img'=2,'ga'=16,'band'=8] {'band'}, dimensions={0} | all-to-all | bytes 3145728 | tf_op jit(solution)/shard_map/all_to_all | solution.py:42
  502.8 0.9 reduce_sum.35
  (47 shorter events, 4.7 us)
Async XLA Ops:
  7.2 81.8 %all-gather.5.cloned.1.call-start = ((), (), s32[]{:S(2)}) async-start(), calls=%async_computation.3 | async-start | bytes 5308416 | tf_op jit(solution)/shard_map/all_gather | solution.py:55
  8.0 127.0 %all-gather.9.cloned.1.call-start = ((), (), s32[]{:S(2)}) async-start(), calls=%async_computation.5 | async-start | bytes 2506752 | tf_op jit(solution)/shard_map/all_gather | solution.py:8
  138.0 45.0 %all-to-all-start = ((bf16[8,96,768]{2,1,0:T(8,128)(2,1)}), bf16[8,96,768]{2,1,0:T(8,128)(2,1)S(1)}, u32[]{:S(2)}, u32[]{:S(2)}) async-start(bf16[8,96,768]{2,1,0:T(8,128)(2,1)} %broadcast_in_dim.5), calls=%async_computation | async-start | bytes 2359296 | tf_op jit(solution)/shard_map/all_to_all | solution.py:14
  144.5 282.2 %all-gather.7.cloned.1.call-start = ((), (), s32[]{:S(2)}) async-start(), calls=%async_computation.4 | async-start | bytes 1769472 | tf_op jit(solution)/shard_map/all_gather | solution.py:56
  187.8 1.5 copy-start.1
  328.4 84.5 %copy-start = (f32[768,768]{1,0:T(8,128)S(1)}, f32[768,768]{1,0:T(8,128)}, u32[]{:S(2)}) copy-start(f32[768,768]{1,0:T(8,128)} %fusion.25) | copy-start | bytes 7077892
  415.0 7.9 %slice-start = ((s8[4718592]{0:T(1024)(128)(4,1)}), s8[4194304]{0:T(1024)(128)(4,1)S(1)}, s32[]{:S(2)}) async-start(s8[4718592]{0:T(1024)(128)(4,1)} %bitcast.90), calls=%async_computation.6 | async-start | bytes 8388608
  417.5 5.4 %slice-start.1 = ((s8[4718592]{0:T(1024)(128)(4,1)}), s8[524288]{0:T(1024)(128)(4,1)S(1)}, s32[]{:S(2)}) async-start(s8[4718592]{0:T(1024)(128)(4,1)} %bitcast.90), calls=%async_computation.7 | async-start | bytes 1048576
  419.5 3.4 copy-start.2
Sparse Core Ops, SparseCore 0:
  9.8 79.1 all-gather.4
  93.9 40.9 all-gather.8
  147.1 44.9 all-gather.6
where the time goes:
time: 515 us; the launch traced here: 511 us
  other arithmetic  193 us (37%)
  waiting for transfers between devices  159 us (31%)
  blocking collectives  70.3 us (14%)
  matrix products  37 us (7%)
  local copies, waits for them, and re-layouts  26.8 us (5%)
  between operations  18.2 us (4%)
  starting transfers between devices  6.6 us (1%)
    another operation x22, other arithmetic, shards(): factor = jnp.linalg.cholesky(margin)  124 us
    all_gather x1, waiting for transfers between devices, shards(): lax.all_gather(orbitals, 'band', axis=0, tiled=True)  80.9 us
    another operation x3, other arithmetic, shards(): lax.linalg.triangular_solve(factor, identity, left_side=True, lower=True)  61.4 us
    all_to_all x1, blocking collectives, sent_and_summed(): lax.all_to_all(pieces, axis, split_axis=0, concat_axis=0, tiled=True)  43 us
    all_gather x1, waiting for transfers between devices, over_pieces(): pieces = lax.all_gather(shard, axis).astype(jnp.float32)  41.2 us
    all_to_all x1, waiting for transfers between devices, from_everyone(): lax.all_to_all(jnp.broadcast_to(shard[None], (count, *shard.shape)), axis...  35.2 us
    all_to_all x1, blocking collectives, from_everyone(): lax.all_to_all(jnp.broadcast_to(shard[None], (count, *shard.shape)), axis...  27.3 us
    another operation x18, local copies, waits for them, and re-layouts  21.5 us
  transfers between devices with their start and end apart: 4, of which 3 were waited for; matrix products, arithmetic and copies ran while one was open for 47% of the time, Pallas kernels for 0%

commit v1 on v0

v1 whole, which is shorter than its diff:
```python
import functools

import jax
import jax.numpy as jnp
from jax import lax
from jax.experimental import pallas as pl
from jax.experimental.pallas import tpu as pltpu
from jax.sharding import Mesh
from jax.sharding import PartitionSpec as P

SUB = 8
BLK = 128
TILE = 512


def split(a):
    hi = a.astype(jnp.bfloat16)
    return hi, (a - hi.astype(jnp.float32)).astype(jnp.bfloat16)


def dot3(a, b, dims):
    (ah, al), (bh, bl) = a, b
    dot = functools.partial(
        lax.dot_general, dimension_numbers=(dims, ((), ())), preferred_element_type=jnp.float32
    )
    return dot(ah, bh) + (dot(ah, bl) + dot(al, bh))


def wide(x):
    return jnp.broadcast_to(x, (SUB, BLK))


def inverse_of_factor(rows, inv):
    sub = lax.broadcasted_iota(jnp.int32, (SUB, BLK), 0)
    for p in range(len(rows)):
        k = p * SUB
        v, g = rows[p], inv[p]
        cols = [wide(v[:, k + j : k + j + 1]) for j in range(SUB)]
        scale, mult, us, gs = [], {}, [], []
        for j in range(SUB):
            r = lax.rsqrt(wide(cols[j][j : j + 1]))
            lj = cols[j] * r
            for m in range(j + 1, SUB):
                mult[j, m] = wide(lj[m : m + 1])
                cols[m] = cols[m] - lj * mult[j, m]
            u, w = wide(v[j : j + 1]) * r, wide(g[j : j + 1]) * r
            below = jnp.where(sub > j, lj, 0.0)
            v = jnp.where(sub == j, u, v - below * u)
            g = jnp.where(sub == j, w, g - below * w)
            scale.append(r)
            us.append(u)
            gs.append(w)
        rows[p], inv[p] = v, g
        for q in range(p + 1, len(rows)):
            c = [wide(rows[q][:, k + j : k + j + 1]) for j in range(SUB)]
            a, b = rows[q], inv[q]
            for j in range(SUB):
                lj = c[j] * scale[j]
                for m in range(j + 1, SUB):
                    c[m] = c[m] - lj * mult[j, m]
                a = a - lj * us[j]
                b = b - lj * gs[j]
            rows[q], inv[q] = a, b
    return inv


def eliminate(a, g_ref, r_ref):
    blocks = a.shape[0] // BLK
    row = lax.broadcasted_iota(jnp.int32, (SUB, BLK), 0)
    col = lax.broadcasted_iota(jnp.int32, (SUB, BLK), 1)

    def step(b, _):
        at = pl.multiple_of(b * BLK, BLK)
        here = pl.ds(at, BLK)
        rows = [
            a[pl.ds(pl.multiple_of(at + SUB * i, SUB), SUB), here] for i in range(BLK // SUB)
        ]
        inv = [jnp.where(col == row + SUB * i, 1.0, 0.0) for i in range(BLK // SUB)]
        for i, g in enumerate(inverse_of_factor(rows, inv)):
            g_ref[SUB * i : SUB * (i + 1), :] = g
        g = g_ref[...]
        r = dot3(split(g), split(a[here, :]), ((1,), (0,)))
        r_ref[...] = r
        a[here, :] = r
        a[here, here] = g
        rb = split(a[here, :])

        def below(i, _):
            them = pl.ds(pl.multiple_of(i * BLK, BLK), BLK)
            update = dot3(split(r_ref[:, them]), rb, ((0,), (0,)))
            a[them, here] = jnp.zeros((BLK, BLK), jnp.float32)
            a[them, :] = a[them, :] - update
            return 0

        lax.fori_loop(b + 1, blocks, below, 0)
        return 0

    lax.fori_loop(0, blocks, step, 0)


def coefficients_kernel(at_ref, m_ref, s_ref, o_ref, a_ref, g_ref, r_ref):
    n = a_ref.shape[0]
    own = o_ref.shape[0] // 2 - s_ref.shape[0]
    a_ref[...] = m_ref[...].astype(jnp.float32)
    eliminate(a_ref, g_ref, r_ref)
    row = lax.broadcasted_iota(jnp.int32, (n, n), 0)
    col = lax.broadcasted_iota(jnp.int32, (n, n), 1)
    a_ref[...] = jnp.where(row >= col, a_ref[...], 0.0)
    inverse = split(a_ref[...])
    coupling = dot3(split(s_ref[...]), inverse, ((1,), (1,)))
    applied = -dot3(split(coupling), inverse, ((1,), (0,)))
    first = pl.multiple_of(at_ref[0] * own, SUB)
    half = o_ref.shape[0] // 2
    hi, lo = split(a_ref[pl.ds(first, own), :])
    o_ref[:own, :] = hi
    o_ref[half : half + own, :] = lo
    hi, lo = split(applied)
    o_ref[own:half, :] = hi
    o_ref[half + own :, :] = lo


def coefficients(at, margin, overlap, own):
    n = margin.shape[0]
    rows = own + overlap.shape[0]
    vmem = pl.BlockSpec(memory_space=pltpu.VMEM)
    return pl.pallas_call(
        coefficients_kernel,
        out_shape=jax.ShapeDtypeStruct((2 * rows, n), jnp.bfloat16),
        in_specs=[pl.BlockSpec(memory_space=pltpu.SMEM), vmem, vmem],
        out_specs=vmem,
        scratch_shapes=[
            pltpu.VMEM((n, n), jnp.float32),
            pltpu.VMEM((BLK, BLK), jnp.float32),
            pltpu.VMEM((BLK, n), jnp.float32),
        ],
        name="coefficients",
    )(at, margin, overlap)


def outputs_kernel(own, c_ref, *refs):
    pieces, (p_ref, x_ref), w_ref = refs[:-3], refs[-3:-1], refs[-1]
    at = 0
    for piece in pieces:
        w_ref[at : at + piece.shape[0], :] = piece[...]
        at += piece.shape[0]
    both = jnp.dot(c_ref[...], w_ref[...], preferred_element_type=jnp.float32)
    half = both.shape[0] // 2
    out = (both[:half] + both[half:]).astype(jnp.bfloat16)
    p_ref[...] = out[:own]
    x_ref[...] = out[own:]


def outputs(coefs, pieces, own):
    half, n = coefs.shape[0] // 2, coefs.shape[1]
    cols = pieces[0].shape[1]
    tile = lambda rows: pl.BlockSpec((rows, TILE), lambda i: (0, i))
    return pl.pallas_call(
        functools.partial(outputs_kernel, own),
        grid=(cols // TILE,),
        in_specs=[pl.BlockSpec(coefs.shape, lambda i: (0, 0))] + [tile(p.shape[0]) for p in pieces],
        out_specs=[tile(own), tile(half - own)],
        out_shape=[
            jax.ShapeDtypeStruct((own, cols), jnp.bfloat16),
            jax.ShapeDtypeStruct((half - own, cols), jnp.bfloat16),
        ],
        scratch_shapes=[pltpu.VMEM((n, TILE), jnp.bfloat16)],
        name="outputs",
    )(coefs, *pieces)


def ring_gather(shard):
    count = lax.axis_size("band")
    right = [(i, (i + 1) % count) for i in range(count)]
    left = [(i, (i - 1) % count) for i in range(count)]
    mid = shard.shape[0] // 2
    halves = [shard[:mid], shard[mid:]]
    got = [[None, None] for _ in range(count)]
    got[0] = list(halves)
    far = count // 2
    moving = {("r", 0): halves[0], ("l", 1): halves[1], ("r", 1): halves[1], ("l", 0): halves[0]}
    for s in range(1, far + 1):
        for (way, h), piece in list(moving.items()):
            if s == far and (way, h) in (("r", 1), ("l", 0)):
                continue
            piece = lax.ppermute(piece, "band", right if way == "r" else left)
            moving[way, h] = piece
            got[(count - s if way == "r" else s) % count][h] = piece
    return got


def to_all(shard, axis):
    count = lax.axis_size(axis)
    return lax.all_to_all(
        jnp.broadcast_to(shard[None], (count, *shard.shape)), axis, 0, 0, tiled=True
    )


def shards(orbitals, kernel, block_vectors):
    band = lax.axis_index("band")
    core = lax.axis_index("core")
    count = lax.axis_size("band")
    total = orbitals.shape[1] * lax.axis_size("y") * lax.axis_size("core")
    own, mine = orbitals.shape[0], block_vectors.shape[0]
    ho, hb = own // 2, mine // 2
    swap = [(0, 1), (1, 0)]

    weighted = (-(orbitals.astype(jnp.float32) * kernel[None, :])).astype(jnp.bfloat16)
    got = ring_gather(weighted)

    left = jnp.concatenate(
        [orbitals[:ho], block_vectors[:hb], orbitals[ho:], block_vectors[hb:]], axis=0
    )
    parts = [
        lax.dot_general(left, half, (((1,), (1,)), ((), ())), preferred_element_type=jnp.float32)
        for pair in got
        for half in pair
    ]
    partial = jnp.concatenate(parts + parts, axis=1)
    n = own * count
    partial = lax.dynamic_slice_in_dim(partial, (count - band) * own, n, 1)

    rows = ho + hb
    kept = lax.dynamic_slice_in_dim(partial, core * rows, rows, 0)
    sent = lax.dynamic_slice_in_dim(partial, (1 - core) * rows, rows, 0)
    kept = kept + lax.ppermute(sent, "core", swap)
    summed = to_all(kept.astype(jnp.bfloat16), "y").astype(jnp.float32).sum(axis=0) / total
    margin_rows = to_all((-summed[:ho]).astype(jnp.bfloat16), "band")
    other_rows = lax.ppermute(margin_rows, "core", swap)
    overlap = summed[ho:]
    other = lax.ppermute(overlap, "core", swap)
    first = core == 0
    margin = jnp.concatenate(
        [
            jnp.where(first, margin_rows, other_rows)[:, None],
            jnp.where(first, other_rows, margin_rows)[:, None],
        ],
        axis=1,
    ).reshape(n, n)
    overlap = jnp.concatenate(
        [jnp.where(first, overlap, other), jnp.where(first, other, overlap)], axis=0
    )
    coefs = coefficients(band[None], margin, overlap, own)
    coefs = lax.dynamic_slice_in_dim(
        jnp.concatenate([coefs, coefs], axis=1), band * own, n, 1
    )
    return tuple(outputs(coefs, [half for pair in got for half in pair], own))


def solution(mesh):
    images, ga, bands = (mesh.shape[a] for a in ("img", "ga", "band"))
    split_mesh = Mesh(
        mesh.devices.reshape(images, ga // 2, 2, bands), ("img", "y", "core", "band")
    )
    rows, cols = ("img", "band"), ("y", "core")
    return jax.shard_map(
        shards,
        mesh=split_mesh,
        in_specs=(P(rows, cols), P(cols), P(rows, cols)),
        out_specs=(P(rows, cols), P(rows, cols)),
        check_vma=False,
    )
```

time: 515 us -> 170 us (0.33)
  other arithmetic: 193 us -> 5.64 us
  waiting for transfers between devices: 159 us -> 20.5 us
  Pallas kernels: 0 us -> 42.1 us
  starting transfers between devices: 6.6 us -> 47.2 us
  matrix products: 37 us -> 5.82 us
  local copies, waits for them, and re-layouts: 26.8 us -> 0.68 us
  blocking collectives: 70.3 us -> 46.3 us
  between operations: 18.2 us -> 1.5 us
    another operation x25 -> x0, other arithmetic: 185 us -> none  [the longest x22 124 us: shards(): factor = jnp.linalg.cholesky(margin)]
    all_gather x3 -> x0, waiting for transfers between devices: 122 us -> none  [the longest x1 80.9 us: shards(): lax.all_gather(orbitals, 'band', axis=0, tiled=True)]
    ppermute x0 -> x17, starting transfers between devices: none -> 47.2 us  [the longest x14 23.2 us: ring_gather(): piece = lax.ppermute(piece, 'band', right if way == 'r' else left)]
    pallas_call x0 -> x2, Pallas kernels: none -> 42.1 us  [the longest x1 36 us: coefficients(): pl.pallas_call(coefficients_kernel, out_shape=jax.ShapeDtypeStruct((2 * r...]
    all_to_all x1 -> x0, waiting for transfers between devices: 35.2 us -> none  [from_everyone(): lax.all_to_all(jnp.broadcast_to(shard[None], (count, *shard.shape)), axis...]
    all_to_all x2, blocking collectives: 70.3 us -> 46.3 us  [to_all(): lax.all_to_all(jnp.broadcast_to(shard[None], (count, *shard.shape)), axis...]
    another operation x21 -> x0, matrix products: 22.9 us -> none  [the longest x11 13.1 us: shards(): lax.linalg.triangular_solve(factor, identity, left_side=True, lower=True)]
    another operation x25 -> x0, local copies, waits for them, and re-layouts: 21.7 us -> none
  transfers between devices with their start and end apart: 4 -> 17, of which waited for: 3 -> 8; matrix products, arithmetic and copies ran while one was open for 47% -> 3% of each run, Pallas kernels for 0% -> 0%
where the time goes in v1:
time: 170 us
  starting transfers between devices  47.2 us (28%)
  blocking collectives  46.3 us (27%)
  Pallas kernels  42.1 us (25%)
  waiting for transfers between devices  20.5 us (12%)
  matrix products  5.82 us (3%)
  other arithmetic  5.64 us (3%)
    all_to_all x2, blocking collectives, to_all(): lax.all_to_all(jnp.broadcast_to(shard[None], (count, *shard.shape)), axis...  46.3 us
    pallas_call x1, Pallas kernels, coefficients(): pl.pallas_call(coefficients_kernel, out_shape=jax.ShapeDtypeStruct((2 * r...  36 us
    ppermute x14, starting transfers between devices, ring_gather(): piece = lax.ppermute(piece, 'band', right if way == 'r' else left)  23.2 us
    ppermute x1, starting transfers between devices, shards(): kept = kept + lax.ppermute(sent, 'core', swap)  19.8 us
    ppermute x14, waiting for transfers between devices, ring_gather(): piece = lax.ppermute(piece, 'band', right if way == 'r' else left)  17.6 us
    pallas_call x1, Pallas kernels, outputs(): pl.pallas_call(functools.partial(outputs_kernel, own), grid=(cols // TILE...  6.07 us
    dot_general x16, matrix products, shards(): lax.dot_general(left, half, (((1,), (1,)), ((), ())), preferred_element_t...  5.82 us
    ppermute x1, starting transfers between devices, shards(): other_rows = lax.ppermute(margin_rows, 'core', swap)  4.06 us
  transfers between devices with their start and end apart: 17, of which 8 were waited for; matrix products, arithmetic and copies ran while one was open for 3% of the time, Pallas kernels for 0%

profile of v1, /device:TPU:513, one launch (start us, length us, event | category | flops | bytes accessed | tf_op | source)
XLA Modules:
  0.0 169.8 jit_solution(7785655312062098339)
XLA Ops:
  0.6 1.3 negate_convert_fusion
  1.9 0.0 copy-start.17
  2.0 4.5 %collective-permute-start = (bf16[48,3072]{1,0:T(8,128)(2,1)S(1)}, bf16[48,3072]{1,0:T(8,128)(2,1)S(1)}, u32[]{:S(2)}, u32[]{:S(2)}) collective-permute-start(bf16[48,3072]{1,0:T(8,128)(2,1)S(1)} %get-tuple-element.5.refs_0_), channel_id=1, source_target_pairs={{0,7},{1,0},{2,1},{3,2},{4,3},{5,4},{6,5},{7,6},{8,15},{9,8},{10,9... | collective-permute-start | bytes 884744 | tf_op jit(solution)/shard_map/ppermute | solution.py:185
  6.5 2.7 %collective-permute-start.1 = (bf16[48,3072]{1,0:T(8,128)(2,1)S(1)}, bf16[48,3072]{1,0:T(8,128)(2,1)S(1)}, u32[]{:S(2)}, u32[]{:S(2)}) collective-permute-start(bf16[48,3072]{1,0:T(8,128)(2,1)S(1)} %get-tuple-element.4.refs_1_), channel_id=1, source_target_pairs={{0,7},{1,0},{2,1},{3,2},{4,3},{5,4},{6,5},{7,6},{8,15},{9,8},{10,9... | collective-permute-start | bytes 884744 | tf_op jit(solution)/shard_map/ppermute | solution.py:185
  9.1 0.0 collective-permute-start.11
  9.2 0.1 pad_maximum_fusion.1
  9.3 0.4 constant_dynamic-update-slice_fusion.31
  9.7 0.4 constant_dynamic-update-slice_fusion.30
  10.1 0.1 collective-permute-done.refs_2_
  10.2 3.1 %collective-permute-start.2 = (bf16[48,3072]{1,0:T(8,128)(2,1)S(1)}, bf16[48,3072]{1,0:T(8,128)(2,1)S(1)}, u32[]{:S(2)}, u32[]{:S(2)}) collective-permute-start(bf16[48,3072]{1,0:T(8,128)(2,1)S(1)} %collective-permute-done.refs_2_), channel_id=1, source_target_pairs={{0,7},{1,0},{2,1},{3,2},{4,3},{5,4},{6,5},{7,6},{8,15},{9,8},{10,9... | collective-permute-start | bytes 884744 | tf_op jit(solution)/shard_map/ppermute | solution.py:185
  13.3 0.0 collective-permute-done.1.refs_3_
  13.4 4.2 %collective-permute-start.3 = (bf16[48,3072]{1,0:T(8,128)(2,1)S(1)}, bf16[48,3072]{1,0:T(8,128)(2,1)S(1)}, u32[]{:S(2)}, u32[]{:S(2)}) collective-permute-start(bf16[48,3072]{1,0:T(8,128)(2,1)S(1)} %collective-permute-done.1.refs_3_), channel_id=1, source_target_pairs={{0,7},{1,0},{2,1},{3,2},{4,3},{5,4},{6,5},{7,6},{8,15},{9,8},{10,9... | collective-permute-start | bytes 884744 | tf_op jit(solution)/shard_map/ppermute | solution.py:185
  17.6 0.4 constant_dynamic-update-slice_fusion.29
  17.9 0.0 collective-permute-done.11.refs_15_
  18.0 2.6 %collective-permute-start.12 = (bf16[48,3072]{1,0:T(8,128)(2,1)S(1)}, bf16[48,3072]{1,0:T(8,128)(2,1)S(1)}, u32[]{:S(2)}, u32[]{:S(2)}) collective-permute-start(bf16[48,3072]{1,0:T(8,128)(2,1)S(1)} %collective-permute-done.11.refs_15_), channel_id=1, source_target_pairs={{0,1},{1,2},{2,3},{3,4},{4,5},{5,6},{6,7},{7,0},{8,9},{9,10},{10,1... | collective-permute-start | bytes 884744 | tf_op jit(solution)/shard_map/ppermute | solution.py:185
  20.5 0.4 constant_dynamic-update-slice_fusion.28
  20.9 0.0 collective-permute-done.2.refs_4_
  20.9 0.8 collective-permute-start.4
  21.7 3.2 %collective-permute-start.5 = (bf16[48,3072]{1,0:T(8,128)(2,1)S(1)}, bf16[48,3072]{1,0:T(8,128)(2,1)S(1)}, u32[]{:S(2)}, u32[]{:S(2)}) collective-permute-start(bf16[48,3072]{1,0:T(8,128)(2,1)S(1)} %collective-permute-done.3.refs_5_), channel_id=1, source_target_pairs={{0,7},{1,0},{2,1},{3,2},{4,3},{5,4},{6,5},{7,6},{8,15},{9,8},{10,9... | collective-permute-start | bytes 884744 | tf_op jit(solution)/shard_map/ppermute | solution.py:185
  24.9 0.4 constant_dynamic-update-slice_fusion.27
  25.2 0.0 copy-done.3
  25.3 4.1 %collective-permute-done.12.refs_13_ = bf16[48,3072]{1,0:T(8,128)(2,1)S(1)} collective-permute-done((bf16[48,3072]{1,0:T(8,128)(2,1)S(1)}, bf16[48,3072]{1,0:T(8,128)(2,1)S(1)}, u32[]{:S(2)}, u32[]{:S(2)}) %collective-permute-start.12) | collective-permute-done | bytes 294944 | tf_op jit(solution)/shard_map/ppermute | solution.py:185
  29.4 0.4 constant_dynamic-update-slice_fusion.26
  29.8 5.9 %collective-permute-done.8.refs_10_ = bf16[48,3072]{1,0:T(8,128)(2,1)S(1)} collective-permute-done((bf16[48,3072]{1,0:T(8,128)(2,1)S(1)}, bf16[48,3072]{1,0:T(8,128)(2,1)S(1)}, u32[]{:S(2)}, u32[]{:S(2)}) %collective-permute-start.8) | collective-permute-done | bytes 294944 | tf_op jit(solution)/shard_map/ppermute | solution.py:185
  35.7 1.0 collective-permute-done.5.refs_7_
  36.7 2.3 %collective-permute-start.10 = (bf16[48,3072]{1,0:T(8,128)(2,1)S(1)}, bf16[48,3072]{1,0:T(8,128)(2,1)S(1)}, u32[]{:S(2)}, u32[]{:S(2)}) collective-permute-start(bf16[48,3072]{1,0:T(8,128)(2,1)S(1)} %collective-permute-done.5.refs_7_), channel_id=1, source_target_pairs={{0,7},{1,0},{2,1},{3,2},{4,3},{5,4},{6,5},{7,6},{8,15},{9,8},{10,9... | collective-permute-start | bytes 884744 | tf_op jit(solution)/shard_map/ppermute | solution.py:185
  39.0 0.4 constant_dynamic-update-slice_fusion.25
  39.4 0.0 copy-done.7
  39.4 0.4 constant_dynamic-update-slice_fusion.24
  39.8 4.9 %collective-permute-done.9.refs_8_ = bf16[48,3072]{1,0:T(8,128)(2,1)S(1)} collective-permute-done((bf16[48,3072]{1,0:T(8,128)(2,1)S(1)}, bf16[48,3072]{1,0:T(8,128)(2,1)S(1)}, u32[]{:S(2)}, u32[]{:S(2)}) %collective-permute-start.9) | collective-permute-done | bytes 294944 | tf_op jit(solution)/shard_map/ppermute | solution.py:185
  44.7 0.4 constant_dynamic-update-slice_fusion.23
  45.1 0.0 copy-done.12
  45.1 1.4 collective-permute-done.10.refs_9_
  46.5 0.4 constant_dynamic-update-slice_fusion.22
  46.9 0.0 copy-done.13
  46.9 0.4 constant_dynamic-update-slice_fusion.21
  47.3 0.0 copy-done.15
  47.3 0.4 constant_dynamic-update-slice_fusion.20
  47.7 0.0 copy-done.16
  47.8 0.4 constant_dynamic-update-slice_fusion.19
  48.1 0.0 copy-done.10
  48.1 0.4 constant_dynamic-update-slice_fusion.18
  48.5 0.0 copy-done.14
  48.6 0.4 constant_dynamic-update-slice_fusion.17
  48.9 0.0 copy-done.6
  48.9 0.4 constant_dynamic-update-slice_fusion.16
  49.5 0.2 dynamic_slice.11
  49.7 19.8 %collective-permute-start.14 = (f32[64,768]{0,1:T(8,128)S(1)}, f32[64,768]{0,1:T(8,128)S(1)}, u32[]{:S(2)}, u32[]{:S(2)}) collective-permute-start(f32[64,768]{0,1:T(8,128)S(1)} %dynamic_slice.11), channel_id=1, source_target_pairs={{0,8},{8,0},{1,9},{9,1},{2,10},{10,2},{3,11},{11,3},{4,12},{12,4},... | collective-permute-start | bytes 589832 | tf_op jit(solution)/shard_map/ppermute | solution.py:225
  69.5 1.3 collective-permute-done.14
  70.8 0.2 add_convert_fusion
  71.0 0.1 copy.7
  71.1 0.1 broadcast_in_dim.11
  71.2 27.1 %all_to_all.10 = bf16[8,64,768]{2,1,0:T(8,128)(2,1)S(1)} all-to-all(bf16[8,64,768]{2,1,0:T(8,128)(2,1)S(1)} %broadcast_in_dim.11), channel_id=1, replica_groups=mesh['img'=2,'y'=8,'core'=2,'band'=8] {'y'}, dimensions={0} | all-to-all | bytes 1572864 | tf_op jit(solution)/shard_map/all_to_all | solution.py:193
  98.3 0.1 convert_reduce_fusion
  98.5 19.2 %all_to_all.11 = bf16[8,48,768]{2,1,0:T(8,128)(2,1)S(1)} all-to-all(bf16[8,48,768]{2,1,0:T(8,128)(2,1)S(1)} %broadcast_in_dim.24), channel_id=1, replica_groups=mesh['img'=2,'y'=8,'core'=2,'band'=8] {'band'}, dimensions={0} | all-to-all | bytes 1179648 | tf_op jit(solution)/shard_map/all_to_all | solution.py:193
  117.7 4.1 %collective-permute-start.15 = (bf16[8,48,768]{2,1,0:T(8,128)(2,1)S(1)}, bf16[8,48,768]{2,1,0:T(8,128)(2,1)S(1)}, u32[]{:S(2)}, u32[]{:S(2)}) collective-permute-start(bf16[8,48,768]{2,1,0:T(8,128)(2,1)S(1)} %all_to_all.11), channel_id=1, source_target_pairs={{0,8},{8,0},{1,9},{9,1},{2,10},{10,2},{3,11},{11,3},{4,12},{12,4},... | collective-permute-start | bytes 1769480 | tf_op jit(solution)/shard_map/ppermute | solution.py:228
  121.8 0.1 collective-permute-start.16
  121.9 1.6 collective-permute-done.16
  123.5 0.6 pad_maximum_fusion.2.s_ref
  124.2 0.1 select_bitcast_fusion.1
  124.3 1.2 pad_maximum_fusion
  125.4 36.0 %coefficients.1 = bf16[256,768]{1,0:T(8,128)(2,1)} custom-call(s32[1]{0:T(128)} %bitcast.at_ref, bf16[768,768]{1,0:T(8,128)(2,1)} %bitcast.38, f32[32,768]{1,0:T(8,128)} %pad_maximum_fusion.2.s_ref), custom_call_target="tpu_custom_call" | custom-call | tf_op jit(solution)/shard_map/coefficients/pallas_call | solution.py:126
  161.5 2.1 %fusion.c_ref = bf16[256,768]{1,0:T(8,128)(2,1)} fusion(s32[]{:T(128)S(6)} %select_n.54, bf16[256,768]{1,0:T(8,128)(2,1)} %coefficients.1), kind=kLoop, calls=%fused_computation.8 | loop fusion | flops 786432 | bytes 786436 | tf_op jit(solution)/shard_map/concatenate | solution.py:244
  163.5 6.1 %outputs.1 = (bf16[96,3072]{1,0:T(8,128)(2,1)}, bf16[32,3072]{1,0:T(8,128)(2,1)}) custom-call(bf16[256,768]{1,0:T(8,128)(2,1)} %fusion.c_ref, bf16[48,3072]{1,0:T(8,128)(2,1)} %copy-done.2, bf16[48,3072]{1,0:T(8,128)(2,1)} %copy-done.1, bf16[48,3072]{1,0:T(8,128)(2,1)} %copy-done.3, bf16[48,3072]{1,0:T(8,128)(2,1)} %copy-done.5, bf16[48,3072]{1,0:T(8,128)(2,1)} %copy-done.7, ...), custom_call_target="tpu_custom_call" | custom-call | tf_op jit(solution)/shard_map/outputs/pallas_call | solution.py:157
  (61 shorter events, 0.3 us)
Async XLA Ops:
  0.6 8.5 %copy-start = (bf16[96,3072]{1,0:T(8,128)(2,1)S(1)}, bf16[96,3072]{1,0:T(8,128)(2,1)}, u32[]{:S(2)}) copy-start(bf16[96,3072]{1,0:T(8,128)(2,1)} %param.3) | copy-start | bytes 1769476
  1.9 7.3 %copy-start.17 = (bf16[32,3072]{1,0:T(8,128)(2,1)S(1)}, bf16[32,3072]{1,0:T(8,128)(2,1)}, u32[]{:S(2)}) copy-start(bf16[32,3072]{1,0:T(8,128)(2,1)} %param.5) | copy-start | bytes 589828
  2.0 7.3 %copy-start.1 = (bf16[48,3072]{1,0:T(8,128)(2,1)}, bf16[48,3072]{1,0:T(8,128)(2,1)S(1)}, u32[]{:S(2)}) copy-start(bf16[48,3072]{1,0:T(8,128)(2,1)S(1)} %get-tuple-element.4.refs_1_) | copy-start | bytes 884740
  2.0 7.3 %copy-start.2 = (bf16[48,3072]{1,0:T(8,128)(2,1)}, bf16[48,3072]{1,0:T(8,128)(2,1)S(1)}, u32[]{:S(2)}) copy-start(bf16[48,3072]{1,0:T(8,128)(2,1)S(1)} %get-tuple-element.5.refs_0_) | copy-start | bytes 884740
  2.0 8.2 %collective-permute-start = (bf16[48,3072]{1,0:T(8,128)(2,1)S(1)}, bf16[48,3072]{1,0:T(8,128)(2,1)S(1)}, u32[]{:S(2)}, u32[]{:S(2)}) collective-permute-start(bf16[48,3072]{1,0:T(8,128)(2,1)S(1)} %get-tuple-element.5.refs_0_), channel_id=1, source_target_pairs={{0,7},{1,0},{2,1},{3,2},{4,3},{5,4},{6,5},{7,6},{8,15},{9,8},{10,9... | collective-permute-start | bytes 884744 | tf_op jit(solution)/shard_map/ppermute | solution.py:185
  6.5 11.1 %collective-permute-start.6 = (bf16[48,3072]{1,0:T(8,128)(2,1)S(1)}, bf16[48,3072]{1,0:T(8,128)(2,1)S(1)}, u32[]{:S(2)}, u32[]{:S(2)}) collective-permute-start(bf16[48,3072]{1,0:T(8,128)(2,1)S(1)} %get-tuple-element.5.refs_0_), channel_id=1, source_target_pairs={{0,1},{1,2},{2,3},{3,4},{4,5},{5,6},{6,7},{7,0},{8,9},{9,10},{10,1... | collective-permute-start | bytes 884744 | tf_op jit(solution)/shard_map/ppermute | solution.py:185
  6.5 6.9 %collective-permute-start.1 = (bf16[48,3072]{1,0:T(8,128)(2,1)S(1)}, bf16[48,3072]{1,0:T(8,128)(2,1)S(1)}, u32[]{:S(2)}, u32[]{:S(2)}) collective-permute-start(bf16[48,3072]{1,0:T(8,128)(2,1)S(1)} %get-tuple-element.4.refs_1_), channel_id=1, source_target_pairs={{0,7},{1,0},{2,1},{3,2},{4,3},{5,4},{6,5},{7,6},{8,15},{9,8},{10,9... | collective-permute-start | bytes 884744 | tf_op jit(solution)/shard_map/ppermute | solution.py:185
  9.1 8.8 %collective-permute-start.11 = (bf16[48,3072]{1,0:T(8,128)(2,1)S(1)}, bf16[48,3072]{1,0:T(8,128)(2,1)S(1)}, u32[]{:S(2)}, u32[]{:S(2)}) collective-permute-start(bf16[48,3072]{1,0:T(8,128)(2,1)S(1)} %get-tuple-element.4.refs_1_), channel_id=1, source_target_pairs={{0,1},{1,2},{2,3},{3,4},{4,5},{5,6},{6,7},{7,0},{8,9},{9,10},{10,1... | collective-permute-start | bytes 884744 | tf_op jit(solution)/shard_map/ppermute | solution.py:185
  10.2 15.1 %copy-start.3 = (bf16[48,3072]{1,0:T(8,128)(2,1)}, bf16[48,3072]{1,0:T(8,128)(2,1)S(1)}, u32[]{:S(2)}) copy-start(bf16[48,3072]{1,0:T(8,128)(2,1)S(1)} %collective-permute-done.refs_2_) | copy-start | bytes 884740
  10.2 10.7 %collective-permute-start.2 = (bf16[48,3072]{1,0:T(8,128)(2,1)S(1)}, bf16[48,3072]{1,0:T(8,128)(2,1)S(1)}, u32[]{:S(2)}, u32[]{:S(2)}) collective-permute-start(bf16[48,3072]{1,0:T(8,128)(2,1)S(1)} %collective-permute-done.refs_2_), channel_id=1, source_target_pairs={{0,7},{1,0},{2,1},{3,2},{4,3},{5,4},{6,5},{7,6},{8,15},{9,8},{10,9... | collective-permute-start | bytes 884744 | tf_op jit(solution)/shard_map/ppermute | solution.py:185
  13.4 11.9 %copy-start.5 = (bf16[48,3072]{1,0:T(8,128)(2,1)}, bf16[48,3072]{1,0:T(8,128)(2,1)S(1)}, u32[]{:S(2)}) copy-start(bf16[48,3072]{1,0:T(8,128)(2,1)S(1)} %collective-permute-done.1.refs_3_) | copy-start | bytes 884740
  13.4 8.3 %collective-permute-start.3 = (bf16[48,3072]{1,0:T(8,128)(2,1)S(1)}, bf16[48,3072]{1,0:T(8,128)(2,1)S(1)}, u32[]{:S(2)}, u32[]{:S(2)}) collective-permute-start(bf16[48,3072]{1,0:T(8,128)(2,1)S(1)} %collective-permute-done.1.refs_3_), channel_id=1, source_target_pairs={{0,7},{1,0},{2,1},{3,2},{4,3},{5,4},{6,5},{7,6},{8,15},{9,8},{10,9... | collective-permute-start | bytes 884744 | tf_op jit(solution)/shard_map/ppermute | solution.py:185
  17.5 31.0 %copy-start.4 = (bf16[48,3072]{1,0:T(8,128)(2,1)}, bf16[48,3072]{1,0:T(8,128)(2,1)S(1)}, u32[]{:S(2)}) copy-start(bf16[48,3072]{1,0:T(8,128)(2,1)S(1)} %collective-permute-done.6.refs_14_) | copy-start | bytes 884740
  17.6 7.3 %collective-permute-start.7 = (bf16[48,3072]{1,0:T(8,128)(2,1)S(1)}, bf16[48,3072]{1,0:T(8,128)(2,1)S(1)}, u32[]{:S(2)}, u32[]{:S(2)}) collective-permute-start(bf16[48,3072]{1,0:T(8,128)(2,1)S(1)} %collective-permute-done.6.refs_14_), channel_id=1, source_target_pairs={{0,1},{1,2},{2,3},{3,4},{4,5},{5,6},{6,7},{7,0},{8,9},{9,10},{10,1... | collective-permute-start | bytes 884744 | tf_op jit(solution)/shard_map/ppermute | solution.py:185
  17.9 31.0 %copy-start.6 = (bf16[48,3072]{1,0:T(8,128)(2,1)}, bf16[48,3072]{1,0:T(8,128)(2,1)S(1)}, u32[]{:S(2)}) copy-start(bf16[48,3072]{1,0:T(8,128)(2,1)S(1)} %collective-permute-done.11.refs_15_) | copy-start | bytes 884740
  18.0 11.4 %collective-permute-start.12 = (bf16[48,3072]{1,0:T(8,128)(2,1)S(1)}, bf16[48,3072]{1,0:T(8,128)(2,1)S(1)}, u32[]{:S(2)}, u32[]{:S(2)}) collective-permute-start(bf16[48,3072]{1,0:T(8,128)(2,1)S(1)} %collective-permute-done.11.refs_15_), channel_id=1, source_target_pairs={{0,1},{1,2},{2,3},{3,4},{4,5},{5,6},{6,7},{7,0},{8,9},{9,10},{10,1... | collective-permute-start | bytes 884744 | tf_op jit(solution)/shard_map/ppermute | solution.py:185
  20.9 18.4 %copy-start.7 = (bf16[48,3072]{1,0:T(8,128)(2,1)}, bf16[48,3072]{1,0:T(8,128)(2,1)S(1)}, u32[]{:S(2)}) copy-start(bf16[48,3072]{1,0:T(8,128)(2,1)S(1)} %collective-permute-done.2.refs_4_) | copy-start | bytes 884740
  20.9 18.0 %collective-permute-start.4 = (bf16[48,3072]{1,0:T(8,128)(2,1)S(1)}, bf16[48,3072]{1,0:T(8,128)(2,1)S(1)}, u32[]{:S(2)}, u32[]{:S(2)}) collective-permute-start(bf16[48,3072]{1,0:T(8,128)(2,1)S(1)} %collective-permute-done.2.refs_4_), channel_id=1, source_target_pairs={{0,7},{1,0},{2,1},{3,2},{4,3},{5,4},{6,5},{7,6},{8,15},{9,8},{10,9... | collective-permute-start | bytes 884744 | tf_op jit(solution)/shard_map/ppermute | solution.py:185
  21.7 17.7 %copy-start.8 = (bf16[48,3072]{1,0:T(8,128)(2,1)}, bf16[48,3072]{1,0:T(8,128)(2,1)S(1)}, u32[]{:S(2)}) copy-start(bf16[48,3072]{1,0:T(8,128)(2,1)S(1)} %collective-permute-done.3.refs_5_) | copy-start | bytes 884740
  21.7 15.0 %collective-permute-start.5 = (bf16[48,3072]{1,0:T(8,128)(2,1)S(1)}, bf16[48,3072]{1,0:T(8,128)(2,1)S(1)}, u32[]{:S(2)}, u32[]{:S(2)}) collective-permute-start(bf16[48,3072]{1,0:T(8,128)(2,1)S(1)} %collective-permute-done.3.refs_5_), channel_id=1, source_target_pairs={{0,7},{1,0},{2,1},{3,2},{4,3},{5,4},{6,5},{7,6},{8,15},{9,8},{10,9... | collective-permute-start | bytes 884744 | tf_op jit(solution)/shard_map/ppermute | solution.py:185
  24.9 22.9 %copy-start.9 = (bf16[48,3072]{1,0:T(8,128)(2,1)}, bf16[48,3072]{1,0:T(8,128)(2,1)S(1)}, u32[]{:S(2)}) copy-start(bf16[48,3072]{1,0:T(8,128)(2,1)S(1)} %collective-permute-done.7.refs_12_) | copy-start | bytes 884740
  24.9 10.8 %collective-permute-start.8 = (bf16[48,3072]{1,0:T(8,128)(2,1)S(1)}, bf16[48,3072]{1,0:T(8,128)(2,1)S(1)}, u32[]{:S(2)}, u32[]{:S(2)}) collective-permute-start(bf16[48,3072]{1,0:T(8,128)(2,1)S(1)} %collective-permute-done.7.refs_12_), channel_id=1, source_target_pairs={{0,1},{1,2},{2,3},{3,4},{4,5},{5,6},{6,7},{7,0},{8,9},{9,10},{10,1... | collective-permute-start | bytes 884744 | tf_op jit(solution)/shard_map/ppermute | solution.py:185
  29.4 18.8 %copy-start.10 = (bf16[48,3072]{1,0:T(8,128)(2,1)}, bf16[48,3072]{1,0:T(8,128)(2,1)S(1)}, u32[]{:S(2)}) copy-start(bf16[48,3072]{1,0:T(8,128)(2,1)S(1)} %collective-permute-done.12.refs_13_) | copy-start | bytes 884740
  29.4 18.0 %collective-permute-start.13 = (bf16[48,3072]{1,0:T(8,128)(2,1)S(1)}, bf16[48,3072]{1,0:T(8,128)(2,1)S(1)}, u32[]{:S(2)}, u32[]{:S(2)}) collective-permute-start(bf16[48,3072]{1,0:T(8,128)(2,1)S(1)} %collective-permute-done.12.refs_13_), channel_id=1, source_target_pairs={{0,1},{1,2},{2,3},{3,4},{4,5},{5,6},{6,7},{7,0},{8,9},{9,10},{10,1... | collective-permute-start | bytes 884744 | tf_op jit(solution)/shard_map/ppermute | solution.py:185
  35.7 11.2 %copy-start.13 = (bf16[48,3072]{1,0:T(8,128)(2,1)}, bf16[48,3072]{1,0:T(8,128)(2,1)S(1)}, u32[]{:S(2)}) copy-start(bf16[48,3072]{1,0:T(8,128)(2,1)S(1)} %collective-permute-done.8.refs_10_) | copy-start | bytes 884740
  35.7 9.0 %collective-permute-start.9 = (bf16[48,3072]{1,0:T(8,128)(2,1)S(1)}, bf16[48,3072]{1,0:T(8,128)(2,1)S(1)}, u32[]{:S(2)}, u32[]{:S(2)}) collective-permute-start(bf16[48,3072]{1,0:T(8,128)(2,1)S(1)} %collective-permute-done.8.refs_10_), channel_id=1, source_target_pairs={{0,1},{1,2},{2,3},{3,4},{4,5},{5,6},{6,7},{7,0},{8,9},{9,10},{10,1... | collective-permute-start | bytes 884744 | tf_op jit(solution)/shard_map/ppermute | solution.py:185
  36.7 8.4 %copy-start.12 = (bf16[48,3072]{1,0:T(8,128)(2,1)}, bf16[48,3072]{1,0:T(8,128)(2,1)S(1)}, u32[]{:S(2)}) copy-start(bf16[48,3072]{1,0:T(8,128)(2,1)S(1)} %collective-permute-done.5.refs_7_) | copy-start | bytes 884740
  36.7 9.8 %collective-permute-start.10 = (bf16[48,3072]{1,0:T(8,128)(2,1)S(1)}, bf16[48,3072]{1,0:T(8,128)(2,1)S(1)}, u32[]{:S(2)}, u32[]{:S(2)}) collective-permute-start(bf16[48,3072]{1,0:T(8,128)(2,1)S(1)} %collective-permute-done.5.refs_7_), channel_id=1, source_target_pairs={{0,7},{1,0},{2,1},{3,2},{4,3},{5,4},{6,5},{7,6},{8,15},{9,8},{10,9... | collective-permute-start | bytes 884744 | tf_op jit(solution)/shard_map/ppermute | solution.py:185
  39.0 6.1 %copy-start.11 = (bf16[48,3072]{1,0:T(8,128)(2,1)}, bf16[48,3072]{1,0:T(8,128)(2,1)S(1)}, u32[]{:S(2)}) copy-start(bf16[48,3072]{1,0:T(8,128)(2,1)S(1)} %collective-permute-done.4.refs_6_) | copy-start | bytes 884740
  44.7 2.6 %copy-start.15 = (bf16[48,3072]{1,0:T(8,128)(2,1)}, bf16[48,3072]{1,0:T(8,128)(2,1)S(1)}, u32[]{:S(2)}) copy-start(bf16[48,3072]{1,0:T(8,128)(2,1)S(1)} %collective-permute-done.9.refs_8_) | copy-start | bytes 884740
  46.5 1.2 copy-start.16
  47.3 1.2 copy-start.14
  49.7 21.1 %collective-permute-start.14 = (f32[64,768]{0,1:T(8,128)S(1)}, f32[64,768]{0,1:T(8,128)S(1)}, u32[]{:S(2)}, u32[]{:S(2)}) collective-permute-start(f32[64,768]{0,1:T(8,128)S(1)} %dynamic_slice.11), channel_id=1, source_target_pairs={{0,8},{8,0},{1,9},{9,1},{2,10},{10,2},{3,11},{11,3},{4,12},{12,4},... | collective-permute-start | bytes 589832 | tf_op jit(solution)/shard_map/ppermute | solution.py:225
  117.7 6.4 %collective-permute-start.15 = (bf16[8,48,768]{2,1,0:T(8,128)(2,1)S(1)}, bf16[8,48,768]{2,1,0:T(8,128)(2,1)S(1)}, u32[]{:S(2)}, u32[]{:S(2)}) collective-permute-start(bf16[8,48,768]{2,1,0:T(8,128)(2,1)S(1)} %all_to_all.11), channel_id=1, source_target_pairs={{0,8},{8,0},{1,9},{9,1},{2,10},{10,2},{3,11},{11,3},{4,12},{12,4},... | collective-permute-start | bytes 1769480 | tf_op jit(solution)/shard_map/ppermute | solution.py:228
  121.8 1.7 collective-permute-start.16

commit v2 on v1

v2 whole, which is shorter than its diff:
```python
import functools

import jax
import jax.numpy as jnp
from jax import lax
from jax.experimental import pallas as pl
from jax.experimental.pallas import tpu as pltpu
from jax.sharding import Mesh
from jax.sharding import PartitionSpec as P

SUB = 8
BLK = 128
TILE = 512


def split(a):
    hi = a.astype(jnp.bfloat16)
    return hi, (a - hi.astype(jnp.float32)).astype(jnp.bfloat16)


def dot3(a, b, dims):
    (ah, al), (bh, bl) = a, b
    dot = functools.partial(
        lax.dot_general, dimension_numbers=(dims, ((), ())), preferred_element_type=jnp.float32
    )
    return dot(ah, bh) + (dot(ah, bl) + dot(al, bh))


def wide(x):
    return jnp.broadcast_to(x, (SUB, BLK))


def lanes(x, k):
    return [wide(x[:, k + j : k + j + 1]) for j in range(SUB)]


def total_of(terms):
    while len(terms) > 1:
        odd = [terms[-1]] if len(terms) % 2 else []
        terms = [a + b for a, b in zip(terms[::2], terms[1::2])] + odd
    return terms[0]


def inverse_of_factor(rows, inv):
    sub = lax.broadcasted_iota(jnp.int32, (SUB, BLK), 0)
    at = [sub == j for j in range(SUB)]
    cols = lanes(rows[0], 0)
    for p in range(len(rows)):
        k = p * SUB
        v, g = rows[p], inv[p]
        last = p + 1 == len(rows)
        if not last:
            ahead, below = lanes(rows[p + 1], k + SUB), lanes(rows[p + 1], k)
        out, unit, recips = g, {}, []
        for j in range(SUB):
            pivot, cj = wide(cols[j][j : j + 1]), cols[j]
            recip = 1.0 / pivot
            recips.append(recip)
            for m in range(j + 1, SUB):
                t = wide(cols[m][j : j + 1]) * recip
                unit[j, m] = t
                cols[m] = jnp.where(at[j], t, cols[m] - cj * t)
            gj = wide(g[j : j + 1])
            out = jnp.where(at[j], gj * lax.rsqrt(pivot), out)
            vj, gj = wide(v[j : j + 1]) * recip, gj * recip
            v = jnp.where(at[j], vj, v - cj * vj)
            g = jnp.where(at[j], gj, g - cj * gj)
        inv[p] = out
        if last:
            break
        lower = list(below)
        for j in range(SUB):
            for m in range(j + 1, SUB):
                lower[m] = lower[m] - lower[j] * unit[j, m]
        scaled = [lower[j] * recips[j] for j in range(SUB)]
        cols = [
            ahead[m] - total_of([lower[j] * wide(scaled[j][m : m + 1]) for j in range(SUB)])
            for m in range(SUB)
        ]
        vs = [wide(v[j : j + 1]) for j in range(SUB)]
        gs = [wide(g[j : j + 1]) for j in range(SUB)]
        for q in range(p + 1, len(rows)):
            c = below if q == p + 1 else lanes(rows[q], k)
            rows[q] = rows[q] - total_of([c[j] * vs[j] for j in range(SUB)])
            inv[q] = inv[q] - total_of([c[j] * gs[j] for j in range(SUB)])
    return inv


def eliminate(a, d_ref, g_ref, r_ref):
    blocks = a.shape[0] // BLK
    row = lax.broadcasted_iota(jnp.int32, (SUB, BLK), 0)
    col = lax.broadcasted_iota(jnp.int32, (SUB, BLK), 1)
    groups = range(BLK // SUB)
    rows_of = ((0,), (0,))

    def block(i):
        return pl.ds(pl.multiple_of(i * BLK, BLK), BLK)

    d_ref[...] = a[:BLK, :BLK]
    r_ref[...] = jnp.zeros(r_ref.shape, jnp.float32)

    def step(b, _):
        rows = [d_ref[SUB * i : SUB * (i + 1), :] for i in groups]
        inv = [jnp.where(col == row + SUB * i, 1.0, 0.0) for i in groups]
        for i, g in enumerate(inverse_of_factor(rows, inv)):
            g_ref[SUB * i : SUB * (i + 1), :] = g
        r = split(r_ref[...])
        before = block(lax.rem(b + blocks - 1, blocks))
        for i in range(blocks - 1):
            them = block(lax.rem(b + i, blocks))
            live = jnp.logical_and(b > 0, b + i < blocks)
            factor = jnp.where(live, r_ref[:, them], 0.0)
            a[them, before] = jnp.where(live, 0.0, a[them, before])
            a[them, :] = a[them, :] - dot3(split(factor), r, rows_of)
        here, after = block(b), block(jnp.minimum(b + 1, blocks - 1))
        g = g_ref[...]
        r_ref[...] = dot3(split(g), split(a[here, :]), ((1,), (0,)))
        factor = split(r_ref[:, after])
        d_ref[...] = a[after, after] - dot3(factor, factor, rows_of)
        r_ref[:, here] = g
        a[here, :] = r_ref[...]
        return 0

    lax.fori_loop(0, blocks, step, 0)


def project_kernel(count, *refs):
    pieces = refs[4 : 4 + 2 * count]
    where_ref, mine_ref, other_ref, s_ref = refs[:4]
    p_ref, x_ref, w_ref, a_ref, b_ref, d_ref, g_ref, r_ref, sem = refs[4 + 2 * count :]
    n, own = a_ref.shape[0], p_ref.shape[0]
    half = own // 2
    band, core = where_ref[0], where_ref[1]

    copies = []
    for i, piece in enumerate(pieces):
        to = lax.rem(band + i // 2, count) * own + (i % 2) * half
        to = pl.multiple_of(to, 2 * SUB)
        copies.append(pltpu.make_async_copy(piece, w_ref.at[pl.ds(to, half), :], sem.at[i]))
        copies[-1].start()

    far = count // 2
    used = (far + 1) * own
    lane = lax.broadcasted_iota(jnp.int32, (half, mine_ref.shape[2]), 1)
    pad = jnp.zeros((half, n - mine_ref.shape[2]), jnp.float32)
    for x in range(count):
        for h in range(2):
            mine, other = mine_ref[x].astype(jnp.float32), other_ref[x].astype(jnp.float32)
            rows = jnp.where(core == h, mine, other)
            rows = jnp.concatenate([jnp.where(lane < used, rows, 0.0), pad], axis=1)
            shift = ((x - far) * own) % n
            if shift:
                rows = pltpu.roll(rows, shift, 1)
            at = x * own + h * half
            b_ref[at : at + half, :] = rows
    for i in range(0, n, BLK):
        for j in range(0, n, BLK):
            a_ref[i : i + BLK, j : j + BLK] = (
                b_ref[i : i + BLK, j : j + BLK] + b_ref[j : j + BLK, i : i + BLK].T
            )

    eliminate(a_ref, d_ref, g_ref, r_ref)

    row = lax.broadcasted_iota(jnp.int32, (n, n), 0)
    col = lax.broadcasted_iota(jnp.int32, (n, n), 1)
    a_ref[...] = jnp.where(row >= col, a_ref[...], 0.0)
    inverse = split(a_ref[...])
    overlap = pltpu.roll(s_ref[...], lax.rem(band + far, count) * own, 1)
    coupling = dot3(split(overlap), inverse, ((1,), (1,)))
    applied = -dot3(split(coupling), inverse, ((1,), (0,)))
    own_rows = a_ref[pl.ds(pl.multiple_of(band * own, SUB), own), :]
    hi, lo = split(jnp.concatenate([own_rows, applied], axis=0))
    both = jnp.concatenate([hi, lo], axis=0)

    for copy in copies:
        copy.wait()
    rows = hi.shape[0]
    for at in range(0, w_ref.shape[1], TILE):
        out = jnp.dot(both, w_ref[:, at : at + TILE], preferred_element_type=jnp.float32)
        out = (out[:rows] + out[rows:]).astype(jnp.bfloat16)
        p_ref[:, at : at + TILE] = out[:own]
        x_ref[:, at : at + TILE] = out[own:]


def project(where, mine, other, overlap, pieces, own):
    count = mine.shape[0]
    n, cols = count * own, pieces[0].shape[1]
    vmem = pl.BlockSpec(memory_space=pltpu.VMEM)
    return pl.pallas_call(
        functools.partial(project_kernel, count),
        out_shape=[
            jax.ShapeDtypeStruct((own, cols), jnp.bfloat16),
            jax.ShapeDtypeStruct((overlap.shape[0], cols), jnp.bfloat16),
        ],
        in_specs=[pl.BlockSpec(memory_space=pltpu.SMEM), vmem, vmem, vmem]
        + [pl.BlockSpec(memory_space=pl.ANY)] * len(pieces),
        out_specs=[vmem, vmem],
        scratch_shapes=[
            pltpu.VMEM((n, cols), jnp.bfloat16),
            pltpu.VMEM((n, n), jnp.float32),
            pltpu.VMEM((n, n), jnp.float32),
            pltpu.VMEM((BLK, BLK), jnp.float32),
            pltpu.VMEM((BLK, BLK), jnp.float32),
            pltpu.VMEM((BLK, n), jnp.float32),
            pltpu.SemaphoreType.DMA((len(pieces),)),
        ],
        name="project",
    )(where, mine, other, overlap, *pieces)


def ring(shard, left):
    count = lax.axis_size("band")
    ways = {s: [(i, (i + s) % count) for i in range(count)] for s in (1, -1)}
    mid = shard.shape[0] // 2
    halves = [shard[:mid], shard[mid:]]
    far = count // 2

    def dot(piece):
        return lax.dot_general(
            left, piece, (((1,), (1,)), ((), ())), preferred_element_type=jnp.float32
        )

    got, parts = {(0, h): halves[h] for h in range(2)}, {}
    moving = {(way, h): halves[h] for way, h in ((1, 0), (-1, 1), (1, 1), (-1, 0))}
    fresh = list(got)
    for s in range(1, far + 1):
        if s == far:
            moving = {key: moving[key] for key in ((1, 0), (-1, 1))}
        moving = {(way, h): lax.ppermute(x, "band", ways[way]) for (way, h), x in moving.items()}
        parts.update({key: dot(got[key]) for key in fresh})
        fresh = [(-way * s % count, h) for way, h in moving]
        got.update(zip(fresh, moving.values()))
    parts.update({key: dot(got[key]) for key in fresh})
    return got, parts


def to_all(shard, axis):
    count = lax.axis_size(axis)
    return lax.all_to_all(
        jnp.broadcast_to(shard[None], (count, *shard.shape)), axis, 0, 0, tiled=True
    )


def shards(orbitals, kernel, block_vectors):
    band, core, count = lax.axis_index("band"), lax.axis_index("core"), lax.axis_size("band")
    total = orbitals.shape[1] * lax.axis_size("y") * lax.axis_size("core")
    own, mine = orbitals.shape[0], block_vectors.shape[0]
    ho, hb = own // 2, mine // 2
    far = count // 2
    swap = [(0, 1), (1, 0)]

    weighted = (-(orbitals.astype(jnp.float32) * kernel[None, :])).astype(jnp.bfloat16)
    left = jnp.concatenate(
        [orbitals[:ho], block_vectors[:hb], orbitals[ho:], block_vectors[hb:]], axis=0
    )
    got, parts = ring(weighted, left)

    order = [((far + i) % count, h) for i in range(count) for h in range(2)]
    partial = jnp.concatenate([parts[key] for key in order], axis=1)
    n = own * count
    rows = ho + hb
    kept = lax.dynamic_slice_in_dim(partial, core * rows, rows, 0)
    sent = lax.dynamic_slice_in_dim(partial, (1 - core) * rows, rows, 0)
    kept = kept + lax.ppermute(sent, "core", swap)

    used = -(-(far + 1) * own // BLK) * BLK
    fold = ho // hb
    cols = n // fold
    packed = jnp.concatenate(
        [
            kept[:ho, :used],
            jnp.concatenate([kept[ho:, i * cols : (i + 1) * cols] for i in range(fold)], axis=0),
        ],
        axis=1,
    )
    summed = to_all(packed.astype(jnp.bfloat16), "y").astype(jnp.float32).sum(axis=0) / total
    column = lax.broadcasted_iota(jnp.int32, (ho, used), 1)
    twice = (column < own) | ((column >= far * own) & (column < (far + 1) * own))
    half_margin = -summed[:, :used] * jnp.where(twice, 0.5, 1.0)
    margin = to_all(half_margin.astype(jnp.bfloat16), "band")
    other_margin = lax.ppermute(margin, "core", swap)
    overlap = jnp.concatenate(
        [summed[i * hb : (i + 1) * hb, used:] for i in range(fold)], axis=1
    )
    other = lax.ppermute(overlap, "core", swap)
    overlap = jnp.where(
        core == 0,
        jnp.concatenate([overlap, other], axis=0),
        jnp.concatenate([other, overlap], axis=0),
    )
    where = jnp.stack([band, core]).astype(jnp.int32)
    pieces = [got[i, h] for i in range(count) for h in range(2)]
    return tuple(project(where, margin, other_margin, overlap, pieces, own))


def solution(mesh):
    images, ga, bands = (mesh.shape[a] for a in ("img", "ga", "band"))
    split_mesh = Mesh(
        mesh.devices.reshape(images, ga // 2, 2, bands), ("img", "y", "core", "band")
    )
    rows, cols = ("img", "band"), ("y", "core")
    return jax.shard_map(
        shards,
        mesh=split_mesh,
        in_specs=(P(rows, cols), P(cols), P(rows, cols)),
        out_specs=(P(rows, cols), P(rows, cols)),
        check_vma=False,
    )
```

time: 170 us -> 156 us (0.918)
  blocking collectives: 46.3 us -> 0 us
  waiting for transfers between devices: 20.5 us -> 47.6 us
  Pallas kernels: 42.1 us -> 31.5 us
  starting transfers between devices: 47.2 us -> 57 us
  local copies, waits for them, and re-layouts: 0.68 us -> 5.41 us
  matrix products: 5.82 us -> 9.86 us
  other arithmetic: 5.64 us -> 2.79 us
    all_to_all x2 -> x0, blocking collectives: 46.3 us -> none  [to_all(): lax.all_to_all(jnp.broadcast_to(shard[None], (count, *shard.shape)), axis...]
    all_to_all x0 -> x2, waiting for transfers between devices: none -> 34.4 us  [to_all(): lax.all_to_all(jnp.broadcast_to(shard[None], (count, *shard.shape)), axis...]
    all_to_all x0 -> x2, starting transfers between devices: none -> 11 us  [to_all(): lax.all_to_all(jnp.broadcast_to(shard[None], (count, *shard.shape)), axis...]
    pallas_call x2 -> x1, Pallas kernels: 42.1 us -> 31.5 us  [project(): pl.pallas_call(functools.partial(project_kernel, count), out_shape=[jax.S...]
    ppermute x15, waiting for transfers between devices: 17.6 us -> 11.3 us  [the longest x14 11.3 us: ring(): lax.ppermute(x, 'band', ways[way])]
    ppermute x15, starting transfers between devices: 27.3 us -> 22.7 us  [the longest x14 22.2 us: ring(): lax.ppermute(x, 'band', ways[way])]
    dot_general x16, matrix products: 5.82 us -> 9.86 us  [dot(): lax.dot_general(left, piece, (((1,), (1,)), ((), ())), preferred_element_...]
    concatenate x4 -> x2, other arithmetic: 3.97 us -> 0.01 us  [the longest x1 0.01 us: shards(): jnp.concatenate([kept[:ho, :used], jnp.concatenate([kept[ho:, i * cols:(i...]
  transfers between devices with their start and end apart: 17 -> 19, of which waited for: 8 -> 11; matrix products, arithmetic and copies ran while one was open for 3% -> 7% of each run, Pallas kernels for 0% -> 0%
where the time goes in v2:
time: 156 us
  starting transfers between devices  57 us (37%)
  waiting for transfers between devices  47.6 us (31%)
  Pallas kernels  31.5 us (20%)
  matrix products  9.86 us (6%)
  local copies, waits for them, and re-layouts  5.41 us (3%)
  other arithmetic  2.79 us (2%)
    all_to_all x2, waiting for transfers between devices, to_all(): lax.all_to_all(jnp.broadcast_to(shard[None], (count, *shard.shape)), axis...  34.4 us
    pallas_call x1, Pallas kernels, project(): pl.pallas_call(functools.partial(project_kernel, count), out_shape=[jax.S...  31.5 us
    ppermute x1, starting transfers between devices, shards(): kept = kept + lax.ppermute(sent, 'core', swap)  22.9 us
    ppermute x14, starting transfers between devices, ring(): lax.ppermute(x, 'band', ways[way])  22.2 us
    ppermute x14, waiting for transfers between devices, ring(): lax.ppermute(x, 'band', ways[way])  11.3 us
    all_to_all x2, starting transfers between devices, to_all(): lax.all_to_all(jnp.broadcast_to(shard[None], (count, *shard.shape)), axis...  11 us
    dot_general x16, matrix products, dot(): lax.dot_general(left, piece, (((1,), (1,)), ((), ())), preferred_element_...  9.86 us
  transfers between devices with their start and end apart: 19, of which 11 were waited for; matrix products, arithmetic and copies ran while one was open for 7% of the time, Pallas kernels for 0%

profile of v2, /device:TPU:513, one launch (start us, length us, event | category | flops | bytes accessed | tf_op | source)
XLA Modules:
  0.0 155.6 jit_solution(9908203867518357411)
XLA Ops:
  0.6 1.2 negate_convert_fusion
  1.9 2.3 %collective-permute-start = (bf16[48,3072]{1,0:T(8,128)(2,1)S(1)}, bf16[48,3072]{1,0:T(8,128)(2,1)S(1)}, u32[]{:S(2)}, u32[]{:S(2)}) collective-permute-start(bf16[48,3072]{1,0:T(8,128)(2,1)S(1)} %get-tuple-element.3.refs_4_), channel_id=1, source_target_pairs={{0,1},{1,2},{2,3},{3,4},{4,5},{5,6},{6,7},{7,0},{8,9},{9,10},{10,1... | collective-permute-start | bytes 884744 | tf_op jit(solution)/shard_map/ppermute | solution.py:229
  4.2 2.3 %collective-permute-start.4 = (bf16[48,3072]{1,0:T(8,128)(2,1)S(1)}, bf16[48,3072]{1,0:T(8,128)(2,1)S(1)}, u32[]{:S(2)}, u32[]{:S(2)}) collective-permute-start(bf16[48,3072]{1,0:T(8,128)(2,1)S(1)} %get-tuple-element.2.refs_5_), channel_id=1, source_target_pairs={{0,7},{1,0},{2,1},{3,2},{4,3},{5,4},{6,5},{7,6},{8,15},{9,8},{10,9... | collective-permute-start | bytes 884744 | tf_op jit(solution)/shard_map/ppermute | solution.py:229
  6.6 4.0 %collective-permute-done.refs_18_ = bf16[48,3072]{1,0:T(8,128)(2,1)S(1)} collective-permute-done((bf16[48,3072]{1,0:T(8,128)(2,1)S(1)}, bf16[48,3072]{1,0:T(8,128)(2,1)S(1)}, u32[]{:S(2)}, u32[]{:S(2)}) %collective-permute-start) | collective-permute-done | bytes 294944 | tf_op jit(solution)/shard_map/ppermute | solution.py:229
  10.5 0.9 collective-permute-start.1
  11.4 3.1 %collective-permute-start.5 = (bf16[48,3072]{1,0:T(8,128)(2,1)S(1)}, bf16[48,3072]{1,0:T(8,128)(2,1)S(1)}, u32[]{:S(2)}, u32[]{:S(2)}) collective-permute-start(bf16[48,3072]{1,0:T(8,128)(2,1)S(1)} %collective-permute-done.4.refs_7_), channel_id=1, source_target_pairs={{0,7},{1,0},{2,1},{3,2},{4,3},{5,4},{6,5},{7,6},{8,15},{9,8},{10,9... | collective-permute-start | bytes 884744 | tf_op jit(solution)/shard_map/ppermute | solution.py:229
  14.5 2.7 %collective-permute-start.11 = (bf16[48,3072]{1,0:T(8,128)(2,1)S(1)}, bf16[48,3072]{1,0:T(8,128)(2,1)S(1)}, u32[]{:S(2)}, u32[]{:S(2)}) collective-permute-start(bf16[48,3072]{1,0:T(8,128)(2,1)S(1)} %get-tuple-element.3.refs_4_), channel_id=1, source_target_pairs={{0,7},{1,0},{2,1},{3,2},{4,3},{5,4},{6,5},{7,6},{8,15},{9,8},{10,9... | collective-permute-start | bytes 884744 | tf_op jit(solution)/shard_map/ppermute | solution.py:229
  17.2 1.3 collective-permute-done.1.refs_16_
  18.5 2.8 %collective-permute-start.6 = (bf16[48,3072]{1,0:T(8,128)(2,1)S(1)}, bf16[48,3072]{1,0:T(8,128)(2,1)}, u32[]{:S(2)}, u32[]{:S(2)}) collective-permute-start(bf16[48,3072]{1,0:T(8,128)(2,1)S(1)} %collective-permute-done.5.refs_9_), channel_id=1, source_target_pairs={{0,7},{1,0},{2,1},{3,2},{4,3},{5,4},{6,5},{7,6},{8,15},{9,8},{10,9... | collective-permute-start | bytes 884744 | tf_op jit(solution)/shard_map/ppermute | solution.py:229
  21.3 0.9 fusion.8
  22.2 0.1 collective-permute-start.9
  22.3 2.6 %collective-permute-start.12 = (bf16[48,3072]{1,0:T(8,128)(2,1)S(1)}, bf16[48,3072]{1,0:T(8,128)(2,1)S(1)}, u32[]{:S(2)}, u32[]{:S(2)}) collective-permute-start(bf16[48,3072]{1,0:T(8,128)(2,1)S(1)} %collective-permute-done.11.refs_6_), channel_id=1, source_target_pairs={{0,7},{1,0},{2,1},{3,2},{4,3},{5,4},{6,5},{7,6},{8,15},{9,8},{10,9... | collective-permute-start | bytes 884744 | tf_op jit(solution)/shard_map/ppermute | solution.py:229
  25.0 0.3 collective-permute-done.2.refs_14_
  25.3 0.2 collective-permute-start.3
  25.5 2.7 %collective-permute-start.7 = (bf16[48,3072]{1,0:T(8,128)(2,1)}, bf16[48,3072]{1,0:T(8,128)(2,1)}, u32[]{:S(2)}, u32[]{:S(2)}) collective-permute-start(bf16[48,3072]{1,0:T(8,128)(2,1)} %collective-permute-done.6.refs_11_), channel_id=1, source_target_pairs={{0,7},{1,0},{2,1},{3,2},{4,3},{5,4},{6,5},{7,6},{8,15},{9,8},{10,9... | collective-permute-start | bytes 884744 | tf_op jit(solution)/shard_map/ppermute | solution.py:229
  28.2 3.7 %collective-permute-done.9.refs_17_ = bf16[48,3072]{1,0:T(8,128)(2,1)} collective-permute-done((bf16[48,3072]{1,0:T(8,128)(2,1)S(1)}, bf16[48,3072]{1,0:T(8,128)(2,1)}, u32[]{:S(2)}, u32[]{:S(2)}) %collective-permute-start.9) | collective-permute-done | bytes 294944 | tf_op jit(solution)/shard_map/ppermute | solution.py:229
  31.9 0.2 collective-permute-done.12.refs_8_
  32.1 2.5 %collective-permute-start.13 = (bf16[48,3072]{1,0:T(8,128)(2,1)S(1)}, bf16[48,3072]{1,0:T(8,128)(2,1)S(1)}, u32[]{:S(2)}, u32[]{:S(2)}) collective-permute-start(bf16[48,3072]{1,0:T(8,128)(2,1)S(1)} %collective-permute-done.12.refs_8_), channel_id=1, source_target_pairs={{0,7},{1,0},{2,1},{3,2},{4,3},{5,4},{6,5},{7,6},{8,15},{9,8},{10,9... | collective-permute-start | bytes 884744 | tf_op jit(solution)/shard_map/ppermute | solution.py:229
  34.6 0.8 collective-permute-done.3.refs_12_
  35.4 0.7 copy-done.14
  36.1 1.5 convolution_dynamic-update-slice_fusion.15
  37.6 1.4 convolution_dynamic-update-slice_fusion.14
  39.0 0.4 convolution_dynamic-update-slice_fusion.13
  39.4 1.0 collective-permute-done.10.refs_15_
  40.4 0.4 convolution_dynamic-update-slice_fusion.12
  40.8 0.3 copy-done.15
  41.1 0.4 convolution_dynamic-update-slice_fusion.11
  41.5 1.3 convolution_dynamic-update-slice_fusion.10
  42.8 0.4 convolution_dynamic-update-slice_fusion.9
  43.2 0.0 copy-done.9
  43.2 0.4 convolution_dynamic-update-slice_fusion.8
  43.6 0.4 convolution_dynamic-update-slice_fusion.7
  44.0 0.4 convolution_dynamic-update-slice_fusion.6
  44.4 0.4 convolution_dynamic-update-slice_fusion.5
  44.8 0.4 convolution_dynamic-update-slice_fusion.4
  45.2 0.4 convolution_dynamic-update-slice_fusion.3
  45.6 0.4 convolution_dynamic-update-slice_fusion.2
  45.9 0.0 collective-permute-done.13.refs_10_
  46.0 0.4 convolution_dynamic-update-slice_fusion.1
  46.3 0.3 copy-done.16
  46.7 1.3 convolution_dynamic-update-slice_fusion
  48.0 0.2 constant_dynamic-slice_fusion
  48.2 22.9 %collective-permute-start.14 = (f32[64,768]{0,1:T(8,128)S(1)}, f32[64,768]{0,1:T(8,128)S(1)}, u32[]{:S(2)}, u32[]{:S(2)}) collective-permute-start(f32[64,768]{0,1:T(8,128)S(1)} %constant_dynamic-slice_fusion), channel_id=1, source_target_pairs={{0,8},{8,0},{1,9},{9,1},{2,10},{10,2},{3,11},{11,3},{4,12},{12,4},... | collective-permute-start | bytes 589832 | tf_op jit(solution)/shard_map/ppermute | solution.py:264
  71.0 1.3 collective-permute-done.14
  72.4 0.2 add_convert_fusion
  72.5 0.1 fusion.9
  72.7 0.1 copy.10
  72.8 0.1 copy.11
  72.8 0.1 copy.12
  72.9 0.1 copy.13
  73.1 0.9 broadcast_in_dim.12
  73.9 5.2 %all-to-all-start = ((bf16[8,48,768]{2,1,0:T(8,128)(2,1)}), bf16[8,48,768]{2,1,0:T(8,128)(2,1)S(1)}, u32[]{:S(2)}, u32[]{:S(2)}) async-start(bf16[8,48,768]{2,1,0:T(8,128)(2,1)} %broadcast_in_dim.12), calls=%async_computation | async-start | bytes 1179648 | tf_op jit(solution)/shard_map/all_to_all | solution.py:239
  79.1 19.4 %all-to-all-done = bf16[8,48,768]{2,1,0:T(8,128)(2,1)S(1)} async-done(((bf16[8,48,768]{2,1,0:T(8,128)(2,1)}), bf16[8,48,768]{2,1,0:T(8,128)(2,1)S(1)}, u32[]{:S(2)}, u32[]{:S(2)}) %all-to-all-start) | async-done | bytes 589856 | tf_op jit(solution)/shard_map/all_to_all | solution.py:239
  98.5 0.1 convert_reduce_fusion
  98.6 0.8 broadcast_in_dim.24
  99.4 5.9 %all-to-all-start.1 = ((bf16[8,48,512]{2,1,0:T(8,128)(2,1)}), bf16[8,48,512]{2,1,0:T(8,128)(2,1)S(1)}, u32[]{:S(2)}, u32[]{:S(2)}) async-start(bf16[8,48,512]{2,1,0:T(8,128)(2,1)} %broadcast_in_dim.24), calls=%async_computation.1 | async-start | bytes 786432 | tf_op jit(solution)/shard_map/all_to_all | solution.py:239
  105.2 15.1 %all-to-all-done.1.refs_1_ = bf16[8,48,512]{2,1,0:T(8,128)(2,1)S(1)} async-done(((bf16[8,48,512]{2,1,0:T(8,128)(2,1)}), bf16[8,48,512]{2,1,0:T(8,128)(2,1)S(1)}, u32[]{:S(2)}, u32[]{:S(2)}) %all-to-all-start.1) | async-done | bytes 393248 | tf_op jit(solution)/shard_map/all_to_all | solution.py:239
  120.3 0.6 collective-permute-start.15
  120.9 0.4 collective-permute-start.16
  121.3 0.7 pad_add_fusion.refs_0_
  121.9 0.6 collective-permute-done.16
  122.5 0.6 maximum_select_fusion.refs_3_
  123.1 0.8 copy-done.4
  123.9 31.5 %project.1 = (bf16[96,3072]{1,0:T(8,128)(2,1)}, bf16[32,3072]{1,0:T(8,128)(2,1)}) custom-call(s32[2]{0:T(128)} %pad_add_fusion.refs_0_, bf16[8,48,512]{2,1,0:T(8,128)(2,1)} %copy-done.1, bf16[8,48,512]{2,1,0:T(8,128)(2,1)} %copy-done.4, f32[32,768]{1,0:T(8,128)} %maximum_select_fusion.refs_3_, bf16[48,3072]{1,0:T(8,128)(2,1)} %copy-done.3, ...), custom_call_target="tpu_custom_call" | custom-call | tf_op jit(solution)/shard_map/project/pallas_call | solution.py:189
  (54 shorter events, 0.2 us)
Async XLA Ops:
  1.8 19.4 %copy-start = (bf16[96,3072]{1,0:T(8,128)(2,1)S(1)}, bf16[96,3072]{1,0:T(8,128)(2,1)}, u32[]{:S(2)}) copy-start(bf16[96,3072]{1,0:T(8,128)(2,1)} %param.3) | copy-start | bytes 1769476
  1.9 20.2 %copy-start.2 = (bf16[48,3072]{1,0:T(8,128)(2,1)}, bf16[48,3072]{1,0:T(8,128)(2,1)S(1)}, u32[]{:S(2)}) copy-start(bf16[48,3072]{1,0:T(8,128)(2,1)S(1)} %get-tuple-element.2.refs_5_) | copy-start | bytes 884740
  1.9 20.2 %copy-start.3 = (bf16[48,3072]{1,0:T(8,128)(2,1)}, bf16[48,3072]{1,0:T(8,128)(2,1)S(1)}, u32[]{:S(2)}) copy-start(bf16[48,3072]{1,0:T(8,128)(2,1)S(1)} %get-tuple-element.3.refs_4_) | copy-start | bytes 884740
  1.9 8.6 %collective-permute-start = (bf16[48,3072]{1,0:T(8,128)(2,1)S(1)}, bf16[48,3072]{1,0:T(8,128)(2,1)S(1)}, u32[]{:S(2)}, u32[]{:S(2)}) collective-permute-start(bf16[48,3072]{1,0:T(8,128)(2,1)S(1)} %get-tuple-element.3.refs_4_), channel_id=1, source_target_pairs={{0,1},{1,2},{2,3},{3,4},{4,5},{5,6},{6,7},{7,0},{8,9},{9,10},{10,1... | collective-permute-start | bytes 884744 | tf_op jit(solution)/shard_map/ppermute | solution.py:229
  4.2 24.0 %copy-start.19 = (bf16[32,3072]{1,0:T(8,128)(2,1)S(1)}, bf16[32,3072]{1,0:T(8,128)(2,1)}, u32[]{:S(2)}) copy-start(bf16[32,3072]{1,0:T(8,128)(2,1)} %param.5) | copy-start | bytes 589828
  4.2 7.2 %collective-permute-start.4 = (bf16[48,3072]{1,0:T(8,128)(2,1)S(1)}, bf16[48,3072]{1,0:T(8,128)(2,1)S(1)}, u32[]{:S(2)}, u32[]{:S(2)}) collective-permute-start(bf16[48,3072]{1,0:T(8,128)(2,1)S(1)} %get-tuple-element.2.refs_5_), channel_id=1, source_target_pairs={{0,7},{1,0},{2,1},{3,2},{4,3},{5,4},{6,5},{7,6},{8,15},{9,8},{10,9... | collective-permute-start | bytes 884744 | tf_op jit(solution)/shard_map/ppermute | solution.py:229
  10.5 32.3 %copy-start.5 = (bf16[48,3072]{1,0:T(8,128)(2,1)}, bf16[48,3072]{1,0:T(8,128)(2,1)S(1)}, u32[]{:S(2)}) copy-start(bf16[48,3072]{1,0:T(8,128)(2,1)S(1)} %collective-permute-done.refs_18_) | copy-start | bytes 884740
  10.5 7.9 %collective-permute-start.1 = (bf16[48,3072]{1,0:T(8,128)(2,1)S(1)}, bf16[48,3072]{1,0:T(8,128)(2,1)S(1)}, u32[]{:S(2)}, u32[]{:S(2)}) collective-permute-start(bf16[48,3072]{1,0:T(8,128)(2,1)S(1)} %collective-permute-done.refs_18_), channel_id=1, source_target_pairs={{0,1},{1,2},{2,3},{3,4},{4,5},{5,6},{6,7},{7,0},{8,9},{9,10},{10,1... | collective-permute-start | bytes 884744 | tf_op jit(solution)/shard_map/ppermute | solution.py:229
  11.4 33.3 %copy-start.6 = (bf16[48,3072]{1,0:T(8,128)(2,1)}, bf16[48,3072]{1,0:T(8,128)(2,1)S(1)}, u32[]{:S(2)}) copy-start(bf16[48,3072]{1,0:T(8,128)(2,1)S(1)} %collective-permute-done.4.refs_7_) | copy-start | bytes 884740
  11.4 7.0 %collective-permute-start.5 = (bf16[48,3072]{1,0:T(8,128)(2,1)S(1)}, bf16[48,3072]{1,0:T(8,128)(2,1)S(1)}, u32[]{:S(2)}, u32[]{:S(2)}) collective-permute-start(bf16[48,3072]{1,0:T(8,128)(2,1)S(1)} %collective-permute-done.4.refs_7_), channel_id=1, source_target_pairs={{0,7},{1,0},{2,1},{3,2},{4,3},{5,4},{6,5},{7,6},{8,15},{9,8},{10,9... | collective-permute-start | bytes 884744 | tf_op jit(solution)/shard_map/ppermute | solution.py:229
  14.5 7.7 %collective-permute-start.8 = (bf16[48,3072]{1,0:T(8,128)(2,1)S(1)}, bf16[48,3072]{1,0:T(8,128)(2,1)S(1)}, u32[]{:S(2)}, u32[]{:S(2)}) collective-permute-start(bf16[48,3072]{1,0:T(8,128)(2,1)S(1)} %get-tuple-element.2.refs_5_), channel_id=1, source_target_pairs={{0,1},{1,2},{2,3},{3,4},{4,5},{5,6},{6,7},{7,0},{8,9},{9,10},{10,1... | collective-permute-start | bytes 884744 | tf_op jit(solution)/shard_map/ppermute | solution.py:229
  14.5 7.8 %collective-permute-start.11 = (bf16[48,3072]{1,0:T(8,128)(2,1)S(1)}, bf16[48,3072]{1,0:T(8,128)(2,1)S(1)}, u32[]{:S(2)}, u32[]{:S(2)}) collective-permute-start(bf16[48,3072]{1,0:T(8,128)(2,1)S(1)} %get-tuple-element.3.refs_4_), channel_id=1, source_target_pairs={{0,7},{1,0},{2,1},{3,2},{4,3},{5,4},{6,5},{7,6},{8,15},{9,8},{10,9... | collective-permute-start | bytes 884744 | tf_op jit(solution)/shard_map/ppermute | solution.py:229
  18.5 22.3 %copy-start.7 = (bf16[48,3072]{1,0:T(8,128)(2,1)}, bf16[48,3072]{1,0:T(8,128)(2,1)S(1)}, u32[]{:S(2)}) copy-start(bf16[48,3072]{1,0:T(8,128)(2,1)S(1)} %collective-permute-done.1.refs_16_) | copy-start | bytes 884740
  18.5 6.8 %collective-permute-start.2 = (bf16[48,3072]{1,0:T(8,128)(2,1)S(1)}, bf16[48,3072]{1,0:T(8,128)(2,1)S(1)}, u32[]{:S(2)}, u32[]{:S(2)}) collective-permute-start(bf16[48,3072]{1,0:T(8,128)(2,1)S(1)} %collective-permute-done.1.refs_16_), channel_id=1, source_target_pairs={{0,1},{1,2},{2,3},{3,4},{4,5},{5,6},{6,7},{7,0},{8,9},{9,10},{10,1... | collective-permute-start | bytes 884744 | tf_op jit(solution)/shard_map/ppermute | solution.py:229
  18.5 27.1 %copy-start.8 = (bf16[48,3072]{1,0:T(8,128)(2,1)}, bf16[48,3072]{1,0:T(8,128)(2,1)S(1)}, u32[]{:S(2)}) copy-start(bf16[48,3072]{1,0:T(8,128)(2,1)S(1)} %collective-permute-done.5.refs_9_) | copy-start | bytes 884740
  18.5 7.0 %collective-permute-start.6 = (bf16[48,3072]{1,0:T(8,128)(2,1)S(1)}, bf16[48,3072]{1,0:T(8,128)(2,1)}, u32[]{:S(2)}, u32[]{:S(2)}) collective-permute-start(bf16[48,3072]{1,0:T(8,128)(2,1)S(1)} %collective-permute-done.5.refs_9_), channel_id=1, source_target_pairs={{0,7},{1,0},{2,1},{3,2},{4,3},{5,4},{6,5},{7,6},{8,15},{9,8},{10,9... | collective-permute-start | bytes 884744 | tf_op jit(solution)/shard_map/ppermute | solution.py:229
  22.1 21.1 %copy-start.9 = (bf16[48,3072]{1,0:T(8,128)(2,1)}, bf16[48,3072]{1,0:T(8,128)(2,1)S(1)}, u32[]{:S(2)}) copy-start(bf16[48,3072]{1,0:T(8,128)(2,1)S(1)} %collective-permute-done.8.refs_19_) | copy-start | bytes 884740
  22.2 9.7 %collective-permute-start.9 = (bf16[48,3072]{1,0:T(8,128)(2,1)S(1)}, bf16[48,3072]{1,0:T(8,128)(2,1)}, u32[]{:S(2)}, u32[]{:S(2)}) collective-permute-start(bf16[48,3072]{1,0:T(8,128)(2,1)S(1)} %collective-permute-done.8.refs_19_), channel_id=1, source_target_pairs={{0,1},{1,2},{2,3},{3,4},{4,5},{5,6},{6,7},{7,0},{8,9},{9,10},{10,1... | collective-permute-start | bytes 884744 | tf_op jit(solution)/shard_map/ppermute | solution.py:229
  22.3 22.1 %copy-start.10 = (bf16[48,3072]{1,0:T(8,128)(2,1)}, bf16[48,3072]{1,0:T(8,128)(2,1)S(1)}, u32[]{:S(2)}) copy-start(bf16[48,3072]{1,0:T(8,128)(2,1)S(1)} %collective-permute-done.11.refs_6_) | copy-start | bytes 884740
  22.3 9.8 %collective-permute-start.12 = (bf16[48,3072]{1,0:T(8,128)(2,1)S(1)}, bf16[48,3072]{1,0:T(8,128)(2,1)S(1)}, u32[]{:S(2)}, u32[]{:S(2)}) collective-permute-start(bf16[48,3072]{1,0:T(8,128)(2,1)S(1)} %collective-permute-done.11.refs_6_), channel_id=1, source_target_pairs={{0,7},{1,0},{2,1},{3,2},{4,3},{5,4},{6,5},{7,6},{8,15},{9,8},{10,9... | collective-permute-start | bytes 884744 | tf_op jit(solution)/shard_map/ppermute | solution.py:229
  25.3 10.1 %copy-start.11 = (bf16[48,3072]{1,0:T(8,128)(2,1)}, bf16[48,3072]{1,0:T(8,128)(2,1)S(1)}, u32[]{:S(2)}) copy-start(bf16[48,3072]{1,0:T(8,128)(2,1)S(1)} %collective-permute-done.2.refs_14_) | copy-start | bytes 884740
  25.3 10.1 %collective-permute-start.3 = (bf16[48,3072]{1,0:T(8,128)(2,1)S(1)}, bf16[48,3072]{1,0:T(8,128)(2,1)S(1)}, u32[]{:S(2)}, u32[]{:S(2)}) collective-permute-start(bf16[48,3072]{1,0:T(8,128)(2,1)S(1)} %collective-permute-done.2.refs_14_), channel_id=1, source_target_pairs={{0,1},{1,2},{2,3},{3,4},{4,5},{5,6},{6,7},{7,0},{8,9},{9,10},{10,1... | collective-permute-start | bytes 884744 | tf_op jit(solution)/shard_map/ppermute | solution.py:229
  25.5 12.1 %collective-permute-start.7 = (bf16[48,3072]{1,0:T(8,128)(2,1)}, bf16[48,3072]{1,0:T(8,128)(2,1)}, u32[]{:S(2)}, u32[]{:S(2)}) collective-permute-start(bf16[48,3072]{1,0:T(8,128)(2,1)} %collective-permute-done.6.refs_11_), channel_id=1, source_target_pairs={{0,7},{1,0},{2,1},{3,2},{4,3},{5,4},{6,5},{7,6},{8,15},{9,8},{10,9... | collective-permute-start | bytes 884744 | tf_op jit(solution)/shard_map/ppermute | solution.py:229
  31.9 8.5 %collective-permute-start.10 = (bf16[48,3072]{1,0:T(8,128)(2,1)}, bf16[48,3072]{1,0:T(8,128)(2,1)S(1)}, u32[]{:S(2)}, u32[]{:S(2)}) collective-permute-start(bf16[48,3072]{1,0:T(8,128)(2,1)} %collective-permute-done.9.refs_17_), channel_id=1, source_target_pairs={{0,1},{1,2},{2,3},{3,4},{4,5},{5,6},{6,7},{7,0},{8,9},{9,10},{10,1... | collective-permute-start | bytes 884744 | tf_op jit(solution)/shard_map/ppermute | solution.py:229
  32.1 13.1 %copy-start.13 = (bf16[48,3072]{1,0:T(8,128)(2,1)}, bf16[48,3072]{1,0:T(8,128)(2,1)S(1)}, u32[]{:S(2)}) copy-start(bf16[48,3072]{1,0:T(8,128)(2,1)S(1)} %collective-permute-done.12.refs_8_) | copy-start | bytes 884740
  32.1 13.8 %collective-permute-start.13 = (bf16[48,3072]{1,0:T(8,128)(2,1)S(1)}, bf16[48,3072]{1,0:T(8,128)(2,1)S(1)}, u32[]{:S(2)}, u32[]{:S(2)}) collective-permute-start(bf16[48,3072]{1,0:T(8,128)(2,1)S(1)} %collective-permute-done.12.refs_8_), channel_id=1, source_target_pairs={{0,7},{1,0},{2,1},{3,2},{4,3},{5,4},{6,5},{7,6},{8,15},{9,8},{10,9... | collective-permute-start | bytes 884744 | tf_op jit(solution)/shard_map/ppermute | solution.py:229
  35.4 0.7 copy-start.14
  36.1 1.5 copy-start.17
  36.1 1.5 copy-start.18
  37.6 1.4 copy-start.12
  40.4 0.7 copy-start.15
  45.9 0.7 copy-start.16
  48.2 24.2 %collective-permute-start.14 = (f32[64,768]{0,1:T(8,128)S(1)}, f32[64,768]{0,1:T(8,128)S(1)}, u32[]{:S(2)}, u32[]{:S(2)}) collective-permute-start(f32[64,768]{0,1:T(8,128)S(1)} %constant_dynamic-slice_fusion), channel_id=1, source_target_pairs={{0,8},{8,0},{1,9},{9,1},{2,10},{10,2},{3,11},{11,3},{4,12},{12,4},... | collective-permute-start | bytes 589832 | tf_op jit(solution)/shard_map/ppermute | solution.py:264
  73.9 24.5 %all-to-all-start = ((bf16[8,48,768]{2,1,0:T(8,128)(2,1)}), bf16[8,48,768]{2,1,0:T(8,128)(2,1)S(1)}, u32[]{:S(2)}, u32[]{:S(2)}) async-start(bf16[8,48,768]{2,1,0:T(8,128)(2,1)} %broadcast_in_dim.12), calls=%async_computation | async-start | bytes 1179648 | tf_op jit(solution)/shard_map/all_to_all | solution.py:239
  99.4 20.9 %all-to-all-start.1 = ((bf16[8,48,512]{2,1,0:T(8,128)(2,1)}), bf16[8,48,512]{2,1,0:T(8,128)(2,1)S(1)}, u32[]{:S(2)}, u32[]{:S(2)}) async-start(bf16[8,48,512]{2,1,0:T(8,128)(2,1)} %broadcast_in_dim.24), calls=%async_computation.1 | async-start | bytes 786432 | tf_op jit(solution)/shard_map/all_to_all | solution.py:239
  120.3 2.8 %copy-start.1 = (bf16[8,48,512]{2,1,0:T(8,128)(2,1)}, bf16[8,48,512]{2,1,0:T(8,128)(2,1)S(1)}, u32[]{:S(2)}) copy-start(bf16[8,48,512]{2,1,0:T(8,128)(2,1)S(1)} %all-to-all-done.1.refs_1_) | copy-start | bytes 1179652
  120.3 2.8 %collective-permute-start.15 = (bf16[8,48,512]{2,1,0:T(8,128)(2,1)S(1)}, bf16[8,48,512]{2,1,0:T(8,128)(2,1)S(1)}, u32[]{:S(2)}, u32[]{:S(2)}) collective-permute-start(bf16[8,48,512]{2,1,0:T(8,128)(2,1)S(1)} %all-to-all-done.1.refs_1_), channel_id=1, source_target_pairs={{0,8},{8,0},{1,9},{9,1},{2,10},{10,2},{3,11},{11,3},{4,12},{12,4},... | collective-permute-start | bytes 1179656 | tf_op jit(solution)/shard_map/ppermute | solution.py:281
  120.9 1.6 %collective-permute-start.16 = (f32[16,768]{1,0:T(8,128)S(1)}, f32[16,768]{1,0:T(8,128)S(1)}, u32[]{:S(2)}, u32[]{:S(2)}) collective-permute-start(f32[16,768]{1,0:T(8,128)S(1)} %pad_maximum_fusion.1), channel_id=1, source_target_pairs={{0,8},{8,0},{1,9},{9,1},{2,10},{10,2},{3,11},{11,3},{4,12},{12,4},... | collective-permute-start | bytes 147464 | tf_op jit(solution)/shard_map/ppermute | solution.py:285
  123.1 0.8 copy-start.4

commit v3 on v2

--- a/solution.py
+++ b/solution.py
@@ -125,12 +125,12 @@
 
 
 def project_kernel(count, *refs):
-    pieces = refs[4 : 4 + 2 * count]
-    where_ref, mine_ref, other_ref, s_ref = refs[:4]
-    p_ref, x_ref, w_ref, a_ref, b_ref, d_ref, g_ref, r_ref, sem = refs[4 + 2 * count :]
+    pieces = refs[6 : 6 + 2 * count]
+    band_ref, core_ref, mine_ref, other_ref, s_ref, s_other_ref = refs[:6]
+    p_ref, x_ref, w_ref, a_ref, b_ref, d_ref, g_ref, r_ref, sem = refs[6 + 2 * count :]
     n, own = a_ref.shape[0], p_ref.shape[0]
     half = own // 2
-    band, core = where_ref[0], where_ref[1]
+    band, core = band_ref[0], core_ref[0]
 
     copies = []
     for i, piece in enumerate(pieces):
@@ -165,7 +165,14 @@
     col = lax.broadcasted_iota(jnp.int32, (n, n), 1)
     a_ref[...] = jnp.where(row >= col, a_ref[...], 0.0)
     inverse = split(a_ref[...])
-    overlap = pltpu.roll(s_ref[...], lax.rem(band + far, count) * own, 1)
+    overlap = jnp.concatenate(
+        [
+            jnp.where(core == 0, s_ref[...], s_other_ref[...]),
+            jnp.where(core == 0, s_other_ref[...], s_ref[...]),
+        ],
+        axis=0,
+    )
+    overlap = pltpu.roll(overlap, lax.rem(band + far, count) * own, 1)
     coupling = dot3(split(overlap), inverse, ((1,), (1,)))
     applied = -dot3(split(coupling), inverse, ((1,), (0,)))
     own_rows = a_ref[pl.ds(pl.multiple_of(band * own, SUB), own), :]
@@ -182,7 +189,7 @@
         x_ref[:, at : at + TILE] = out[own:]
 
 
-def project(where, mine, other, overlap, pieces, own):
+def project(band, core, mine, other, overlap, other_overlap, pieces, own):
     count = mine.shape[0]
     n, cols = count * own, pieces[0].shape[1]
     vmem = pl.BlockSpec(memory_space=pltpu.VMEM)
@@ -190,9 +197,10 @@
         functools.partial(project_kernel, count),
         out_shape=[
             jax.ShapeDtypeStruct((own, cols), jnp.bfloat16),
-            jax.ShapeDtypeStruct((overlap.shape[0], cols), jnp.bfloat16),
+            jax.ShapeDtypeStruct((2 * overlap.shape[0], cols), jnp.bfloat16),
         ],
-        in_specs=[pl.BlockSpec(memory_space=pltpu.SMEM), vmem, vmem, vmem]
+        in_specs=[pl.BlockSpec(memory_space=pltpu.SMEM)] * 2
+        + [vmem] * 4
         + [pl.BlockSpec(memory_space=pl.ANY)] * len(pieces),
         out_specs=[vmem, vmem],
         scratch_shapes=[
@@ -205,7 +213,7 @@
             pltpu.SemaphoreType.DMA((len(pieces),)),
         ],
         name="project",
-    )(where, mine, other, overlap, *pieces)
+    )(band[None], core[None], mine, other, overlap, other_overlap, *pieces)
 
 
 def ring(shard, left):
@@ -226,7 +234,11 @@
     for s in range(1, far + 1):
         if s == far:
             moving = {key: moving[key] for key in ((1, 0), (-1, 1))}
-        moving = {(way, h): lax.ppermute(x, "band", ways[way]) for (way, h), x in moving.items()}
+        for way, h in list(moving):
+            x, before = moving[way, h], (-way * (s - 2) % count, h)
+            if s > 1:
+                x, parts[before] = lax.optimization_barrier((x, parts[before]))
+            moving[way, h] = lax.ppermute(x, "band", ways[way])
         parts.update({key: dot(got[key]) for key in fresh})
         fresh = [(-way * s % count, h) for way, h in moving]
         got.update(zip(fresh, moving.values()))
@@ -283,14 +295,8 @@
         [summed[i * hb : (i + 1) * hb, used:] for i in range(fold)], axis=1
     )
     other = lax.ppermute(overlap, "core", swap)
-    overlap = jnp.where(
-        core == 0,
-        jnp.concatenate([overlap, other], axis=0),
-        jnp.concatenate([other, overlap], axis=0),
-    )
-    where = jnp.stack([band, core]).astype(jnp.int32)
     pieces = [got[i, h] for i in range(count) for h in range(2)]
-    return tuple(project(where, margin, other_margin, overlap, pieces, own))
+    return tuple(project(band, core, margin, other_margin, overlap, other, pieces, own))
 
 
 def solution(mesh):

time: 156 us -> 150 us (0.962)
  blocking collectives: 0 us -> 17 us
  starting transfers between devices: 57 us -> 47.8 us
  waiting for transfers between devices: 47.6 us -> 42.4 us
  matrix products: 9.86 us -> 5.75 us
  local copies, waits for them, and re-layouts: 5.41 us -> 2.53 us
    all_to_all x0 -> x1, blocking collectives: none -> 17 us  [to_all(): lax.all_to_all(jnp.broadcast_to(shard[None], (count, *shard.shape)), axis...]
    all_to_all x2 -> x1, waiting for transfers between devices: 34.4 us -> 19.4 us  [to_all(): lax.all_to_all(jnp.broadcast_to(shard[None], (count, *shard.shape)), axis...]
    ppermute x14, waiting for transfers between devices: 11.3 us -> 20.5 us  [ring(): moving[way, h] = lax.ppermute(x, 'band', ways[way])]
    all_to_all x2 -> x1, starting transfers between devices: 11 us -> 3.95 us  [to_all(): lax.all_to_all(jnp.broadcast_to(shard[None], (count, *shard.shape)), axis...]
    ppermute x1, starting transfers between devices: 22.9 us -> 18.2 us  [shards(): kept = kept + lax.ppermute(sent, 'core', swap)]
    dot_general x16, matrix products: 9.86 us -> 5.75 us  [dot(): lax.dot_general(left, piece, (((1,), (1,)), ((), ())), preferred_element_...]
  transfers between devices with their start and end apart: 19 -> 18, of which waited for: 11 -> 8; matrix products, arithmetic and copies ran while one was open for 7% -> 3% of each run, Pallas kernels for 0% -> 0%
where the time goes in v3:
time: 150 us
  starting transfers between devices  47.8 us (32%)
  waiting for transfers between devices  42.4 us (28%)
  Pallas kernels  31.5 us (21%)
  blocking collectives  17 us (11%)
  matrix products  5.75 us (4%)
  local copies, waits for them, and re-layouts  2.53 us (2%)
  other arithmetic  1.56 us (1%)
  between operations  1.56 us (1%)
    pallas_call x1, Pallas kernels, project(): pl.pallas_call(functools.partial(project_kernel, count), out_shape=[jax.S...  31.5 us
    ppermute x14, starting transfers between devices, ring(): moving[way, h] = lax.ppermute(x, 'band', ways[way])  23.2 us
    ppermute x14, waiting for transfers between devices, ring(): moving[way, h] = lax.ppermute(x, 'band', ways[way])  20.5 us
    all_to_all x1, waiting for transfers between devices, to_all(): lax.all_to_all(jnp.broadcast_to(shard[None], (count, *shard.shape)), axis...  19.4 us
    ppermute x1, starting transfers between devices, shards(): kept = kept + lax.ppermute(sent, 'core', swap)  18.2 us
    all_to_all x1, blocking collectives, to_all(): lax.all_to_all(jnp.broadcast_to(shard[None], (count, *shard.shape)), axis...  17 us
    dot_general x16, matrix products, dot(): lax.dot_general(left, piece, (((1,), (1,)), ((), ())), preferred_element_...  5.75 us
    all_to_all x1, starting transfers between devices, to_all(): lax.all_to_all(jnp.broadcast_to(shard[None], (count, *shard.shape)), axis...  3.95 us
  transfers between devices with their start and end apart: 18, of which 8 were waited for; matrix products, arithmetic and copies ran while one was open for 3% of the time, Pallas kernels for 0%

profile of v3, /device:TPU:513, one launch (start us, length us, event | category | flops | bytes accessed | tf_op | source)
XLA Modules:
  0.0 150.1 jit_solution(7802321219789598688)
XLA Ops:
  0.6 1.2 negate_convert_fusion
  1.8 0.0 copy-start
  1.9 0.0 copy-start.20
  1.9 4.5 %collective-permute-start.4 = (bf16[48,3072]{1,0:T(8,128)(2,1)S(1)}, bf16[48,3072]{1,0:T(8,128)(2,1)S(1)}, u32[]{:S(2)}, u32[]{:S(2)}) collective-permute-start(bf16[48,3072]{1,0:T(8,128)(2,1)S(1)} %get-tuple-element.42.refs_7_), channel_id=1, source_target_pairs={{0,7},{1,0},{2,1},{3,2},{4,3},{5,4},{6,5},{7,6},{8,15},{9,8},{10,9... | collective-permute-start | bytes 884744 | tf_op jit(solution)/shard_map/ppermute | solution.py:241
  6.4 2.7 %collective-permute-start.11 = (bf16[48,3072]{1,0:T(8,128)(2,1)S(1)}, bf16[48,3072]{1,0:T(8,128)(2,1)S(1)}, u32[]{:S(2)}, u32[]{:S(2)}) collective-permute-start(bf16[48,3072]{1,0:T(8,128)(2,1)S(1)} %get-tuple-element.43.refs_6_), channel_id=1, source_target_pairs={{0,7},{1,0},{2,1},{3,2},{4,3},{5,4},{6,5},{7,6},{8,15},{9,8},{10,9... | collective-permute-start | bytes 884744 | tf_op jit(solution)/shard_map/ppermute | solution.py:241
  9.2 0.1 pad_maximum_fusion
  9.3 0.4 fusion.7
  9.6 0.4 fusion.5
  10.0 6.3 %collective-permute-done.refs_20_ = bf16[48,3072]{1,0:T(8,128)(2,1)S(1)} collective-permute-done((bf16[48,3072]{1,0:T(8,128)(2,1)S(1)}, bf16[48,3072]{1,0:T(8,128)(2,1)S(1)}, u32[]{:S(2)}, u32[]{:S(2)}) %collective-permute-start) | collective-permute-done | bytes 294944 | tf_op jit(solution)/shard_map/ppermute | solution.py:241
  16.4 3.1 %collective-permute-start.5 = (bf16[48,3072]{1,0:T(8,128)(2,1)S(1)}, bf16[48,3072]{1,0:T(8,128)(2,1)S(1)}, u32[]{:S(2)}, u32[]{:S(2)}) collective-permute-start(bf16[48,3072]{1,0:T(8,128)(2,1)S(1)} %collective-permute-done.4.refs_9_), channel_id=1, source_target_pairs={{0,7},{1,0},{2,1},{3,2},{4,3},{5,4},{6,5},{7,6},{8,15},{9,8},{10,9... | collective-permute-start | bytes 884744 | tf_op jit(solution)/shard_map/ppermute | solution.py:241
  19.5 3.2 %collective-permute-start.12 = (bf16[48,3072]{1,0:T(8,128)(2,1)S(1)}, bf16[48,3072]{1,0:T(8,128)(2,1)S(1)}, u32[]{:S(2)}, u32[]{:S(2)}) collective-permute-start(bf16[48,3072]{1,0:T(8,128)(2,1)S(1)} %collective-permute-done.11.refs_8_), channel_id=1, source_target_pairs={{0,7},{1,0},{2,1},{3,2},{4,3},{5,4},{6,5},{7,6},{8,15},{9,8},{10,9... | collective-permute-start | bytes 884744 | tf_op jit(solution)/shard_map/ppermute | solution.py:241
  22.7 0.4 fusion.14
  23.1 0.4 fusion.16
  23.5 0.0 copy-done.6
  23.5 0.1 collective-permute-start.2
  23.7 0.4 fusion.18
  24.0 0.0 collective-permute-done.5.refs_11_
  24.1 3.3 %collective-permute-start.6 = (bf16[48,3072]{1,0:T(8,128)(2,1)S(1)}, bf16[48,3072]{1,0:T(8,128)(2,1)S(1)}, u32[]{:S(2)}, u32[]{:S(2)}) collective-permute-start(bf16[48,3072]{1,0:T(8,128)(2,1)S(1)} %collective-permute-done.5.refs_11_), channel_id=1, source_target_pairs={{0,7},{1,0},{2,1},{3,2},{4,3},{5,4},{6,5},{7,6},{8,15},{9,8},{10,9... | collective-permute-start | bytes 884744 | tf_op jit(solution)/shard_map/ppermute | solution.py:241
  27.4 0.4 fusion.15
  27.8 0.0 copy-done.8
  27.8 6.7 %collective-permute-done.2.refs_16_ = bf16[48,3072]{1,0:T(8,128)(2,1)S(1)} collective-permute-done((bf16[48,3072]{1,0:T(8,128)(2,1)S(1)}, bf16[48,3072]{1,0:T(8,128)(2,1)S(1)}, u32[]{:S(2)}, u32[]{:S(2)}) %collective-permute-start.2) | collective-permute-done | bytes 294944 | tf_op jit(solution)/shard_map/ppermute | solution.py:241
  34.4 0.4 fusion.17
  34.8 0.0 copy-done.9
  34.8 1.1 collective-permute-done.6.refs_13_
  35.9 3.3 %collective-permute-start.7 = (bf16[48,3072]{1,0:T(8,128)(2,1)S(1)}, bf16[48,3072]{1,0:T(8,128)(2,1)S(1)}, u32[]{:S(2)}, u32[]{:S(2)}) collective-permute-start(bf16[48,3072]{1,0:T(8,128)(2,1)S(1)} %collective-permute-done.6.refs_13_), channel_id=1, source_target_pairs={{0,7},{1,0},{2,1},{3,2},{4,3},{5,4},{6,5},{7,6},{8,15},{9,8},{10,9... | collective-permute-start | bytes 884744 | tf_op jit(solution)/shard_map/ppermute | solution.py:241
  39.2 0.4 fusion.19
  39.5 0.0 collective-permute-done.9.refs_19_
  39.6 0.3 collective-permute-start.10
  39.9 2.6 %collective-permute-start.13 = (bf16[48,3072]{1,0:T(8,128)(2,1)S(1)}, bf16[48,3072]{1,0:T(8,128)(2,1)S(1)}, u32[]{:S(2)}, u32[]{:S(2)}) collective-permute-start(bf16[48,3072]{1,0:T(8,128)(2,1)S(1)} %collective-permute-done.12.refs_10_), channel_id=1, source_target_pairs={{0,7},{1,0},{2,1},{3,2},{4,3},{5,4},{6,5},{7,6},{8,15},{9,8},{10,9... | collective-permute-start | bytes 884744 | tf_op jit(solution)/shard_map/ppermute | solution.py:241
  42.5 0.4 convolution_dynamic-update-slice_fusion.7
  42.9 1.9 %collective-permute-done.7.refs_15_ = bf16[48,3072]{1,0:T(8,128)(2,1)S(1)} collective-permute-done((bf16[48,3072]{1,0:T(8,128)(2,1)S(1)}, bf16[48,3072]{1,0:T(8,128)(2,1)S(1)}, u32[]{:S(2)}, u32[]{:S(2)}) %collective-permute-start.7) | collective-permute-done | bytes 294944 | tf_op jit(solution)/shard_map/ppermute | solution.py:241
  44.8 0.4 convolution_dynamic-update-slice_fusion.6
  45.2 0.0 copy-done.12
  45.2 0.4 convolution_dynamic-update-slice_fusion.5
  45.6 0.0 copy-done.15
  45.6 4.5 %collective-permute-done.10.refs_17_ = bf16[48,3072]{1,0:T(8,128)(2,1)S(1)} collective-permute-done((bf16[48,3072]{1,0:T(8,128)(2,1)S(1)}, bf16[48,3072]{1,0:T(8,128)(2,1)S(1)}, u32[]{:S(2)}, u32[]{:S(2)}) %collective-permute-start.10) | collective-permute-done | bytes 294944 | tf_op jit(solution)/shard_map/ppermute | solution.py:241
  50.1 0.4 convolution_dynamic-update-slice_fusion.4
  50.5 0.4 convolution_dynamic-update-slice_fusion.3
  50.9 0.0 copy-done.16
  51.0 0.4 convolution_dynamic-update-slice_fusion.2
  51.4 0.4 convolution_dynamic-update-slice_fusion.1
  51.7 0.0 copy-done.13
  51.8 0.4 convolution_dynamic-update-slice_fusion
  52.1 0.0 copy-done.17
  52.1 0.2 constant_dynamic-slice_fusion
  52.3 18.2 %collective-permute-start.14 = (f32[64,768]{0,1:T(8,128)S(1)}, f32[64,768]{0,1:T(8,128)S(1)}, u32[]{:S(2)}, u32[]{:S(2)}) collective-permute-start(f32[64,768]{0,1:T(8,128)S(1)} %constant_dynamic-slice_fusion), channel_id=1, source_target_pairs={{0,8},{8,0},{1,9},{9,1},{2,10},{10,2},{3,11},{11,3},{4,12},{12,4},... | collective-permute-start | bytes 589832 | tf_op jit(solution)/shard_map/ppermute | solution.py:276
  70.5 1.3 collective-permute-done.14
  71.9 0.2 add_convert_fusion
  72.1 0.1 fusion.11
  72.2 0.1 copy.10
  72.3 0.1 copy.11
  72.3 0.1 copy.12
  72.4 0.1 copy.13
  72.6 0.9 broadcast_in_dim.29
  73.4 4.0 %all-to-all-start = ((bf16[8,48,768]{2,1,0:T(8,128)(2,1)}), bf16[8,48,768]{2,1,0:T(8,128)(2,1)S(1)}, u32[]{:S(2)}, u32[]{:S(2)}) async-start(bf16[8,48,768]{2,1,0:T(8,128)(2,1)} %broadcast_in_dim.29), calls=%async_computation | async-start | bytes 1179648 | tf_op jit(solution)/shard_map/all_to_all | solution.py:251
  77.4 19.4 %all-to-all-done = bf16[8,48,768]{2,1,0:T(8,128)(2,1)S(1)} async-done(((bf16[8,48,768]{2,1,0:T(8,128)(2,1)}), bf16[8,48,768]{2,1,0:T(8,128)(2,1)S(1)}, u32[]{:S(2)}, u32[]{:S(2)}) %all-to-all-start) | async-done | bytes 589856 | tf_op jit(solution)/shard_map/all_to_all | solution.py:251
  96.7 0.1 convert_reduce_fusion
  96.9 17.0 %all_to_all.10.refs_2_ = bf16[8,48,512]{2,1,0:T(8,128)(2,1)S(1)} all-to-all(bf16[8,48,512]{2,1,0:T(8,128)(2,1)S(1)} %broadcast_in_dim.32), channel_id=1, replica_groups=mesh['img'=2,'y'=8,'core'=2,'band'=8] {'band'}, dimensions={0} | all-to-all | bytes 786432 | tf_op jit(solution)/shard_map/all_to_all | solution.py:251
  113.9 2.1 %collective-permute-start.15 = (bf16[8,48,512]{2,1,0:T(8,128)(2,1)S(1)}, bf16[8,48,512]{2,1,0:T(8,128)(2,1)S(1)}, u32[]{:S(2)}, u32[]{:S(2)}) collective-permute-start(bf16[8,48,512]{2,1,0:T(8,128)(2,1)S(1)} %all_to_all.10.refs_2_), channel_id=1, source_target_pairs={{0,8},{8,0},{1,9},{9,1},{2,10},{10,2},{3,11},{11,3},{4,12},{12,4},... | collective-permute-start | bytes 1179656 | tf_op jit(solution)/shard_map/ppermute | solution.py:293
  116.1 0.4 collective-permute-start.16
  116.4 1.2 collective-permute-done.16.refs_5_
  117.7 0.6 copy-done.21
  118.2 0.2 copy-done.18
  118.4 31.5 %project.1 = (bf16[96,3072]{1,0:T(8,128)(2,1)}, bf16[32,3072]{1,0:T(8,128)(2,1)}) custom-call(s32[1]{0:T(128)} %bitcast.refs_0_, s32[1]{0:T(128)} %bitcast.1.refs_1_, bf16[8,48,512]{2,1,0:T(8,128)(2,1)} %copy-done.1, bf16[8,48,512]{2,1,0:T(8,128)(2,1)} %copy-done.18, f32[16,768]{1,0:T(8,128)} %copy-done.19, f32[16,768]{1,0:T(8,128)} %copy-done.21, ...), custom_call_target="tpu_custom_call" | custom-call | tf_op jit(solution)/shard_map/project/pallas_call | solution.py:196
  (64 shorter events, 0.3 us)
Async XLA Ops:
  1.8 7.3 %copy-start = (bf16[96,3072]{1,0:T(8,128)(2,1)S(1)}, bf16[96,3072]{1,0:T(8,128)(2,1)}, u32[]{:S(2)}) copy-start(bf16[96,3072]{1,0:T(8,128)(2,1)} %param.3) | copy-start | bytes 1769476
  1.9 7.3 %copy-start.2 = (bf16[48,3072]{1,0:T(8,128)(2,1)}, bf16[48,3072]{1,0:T(8,128)(2,1)S(1)}, u32[]{:S(2)}) copy-start(bf16[48,3072]{1,0:T(8,128)(2,1)S(1)} %get-tuple-element.42.refs_7_) | copy-start | bytes 884740
  1.9 7.3 %copy-start.3 = (bf16[48,3072]{1,0:T(8,128)(2,1)}, bf16[48,3072]{1,0:T(8,128)(2,1)S(1)}, u32[]{:S(2)}) copy-start(bf16[48,3072]{1,0:T(8,128)(2,1)S(1)} %get-tuple-element.43.refs_6_) | copy-start | bytes 884740
  1.9 7.2 %copy-start.20 = (bf16[32,3072]{1,0:T(8,128)(2,1)S(1)}, bf16[32,3072]{1,0:T(8,128)(2,1)}, u32[]{:S(2)}) copy-start(bf16[32,3072]{1,0:T(8,128)(2,1)} %param.5) | copy-start | bytes 589828
  1.9 14.4 %collective-permute-start.4 = (bf16[48,3072]{1,0:T(8,128)(2,1)S(1)}, bf16[48,3072]{1,0:T(8,128)(2,1)S(1)}, u32[]{:S(2)}, u32[]{:S(2)}) collective-permute-start(bf16[48,3072]{1,0:T(8,128)(2,1)S(1)} %get-tuple-element.42.refs_7_), channel_id=1, source_target_pairs={{0,7},{1,0},{2,1},{3,2},{4,3},{5,4},{6,5},{7,6},{8,15},{9,8},{10,9... | collective-permute-start | bytes 884744 | tf_op jit(solution)/shard_map/ppermute | solution.py:241
  6.4 13.0 %collective-permute-start.8 = (bf16[48,3072]{1,0:T(8,128)(2,1)S(1)}, bf16[48,3072]{1,0:T(8,128)(2,1)S(1)}, u32[]{:S(2)}, u32[]{:S(2)}) collective-permute-start(bf16[48,3072]{1,0:T(8,128)(2,1)S(1)} %get-tuple-element.42.refs_7_), channel_id=1, source_target_pairs={{0,1},{1,2},{2,3},{3,4},{4,5},{5,6},{6,7},{7,0},{8,9},{9,10},{10,1... | collective-permute-start | bytes 884744 | tf_op jit(solution)/shard_map/ppermute | solution.py:241
  6.4 9.9 %collective-permute-start = (bf16[48,3072]{1,0:T(8,128)(2,1)S(1)}, bf16[48,3072]{1,0:T(8,128)(2,1)S(1)}, u32[]{:S(2)}, u32[]{:S(2)}) collective-permute-start(bf16[48,3072]{1,0:T(8,128)(2,1)S(1)} %get-tuple-element.43.refs_6_), channel_id=1, source_target_pairs={{0,1},{1,2},{2,3},{3,4},{4,5},{5,6},{6,7},{7,0},{8,9},{9,10},{10,1... | collective-permute-start | bytes 884744 | tf_op jit(solution)/shard_map/ppermute | solution.py:241
  6.4 13.1 %collective-permute-start.11 = (bf16[48,3072]{1,0:T(8,128)(2,1)S(1)}, bf16[48,3072]{1,0:T(8,128)(2,1)S(1)}, u32[]{:S(2)}, u32[]{:S(2)}) collective-permute-start(bf16[48,3072]{1,0:T(8,128)(2,1)S(1)} %get-tuple-element.43.refs_6_), channel_id=1, source_target_pairs={{0,7},{1,0},{2,1},{3,2},{4,3},{5,4},{6,5},{7,6},{8,15},{9,8},{10,9... | collective-permute-start | bytes 884744 | tf_op jit(solution)/shard_map/ppermute | solution.py:241
  16.4 7.1 %copy-start.6 = (bf16[48,3072]{1,0:T(8,128)(2,1)}, bf16[48,3072]{1,0:T(8,128)(2,1)S(1)}, u32[]{:S(2)}) copy-start(bf16[48,3072]{1,0:T(8,128)(2,1)S(1)} %collective-permute-done.refs_20_) | copy-start | bytes 884740
  16.4 7.2 %collective-permute-start.1 = (bf16[48,3072]{1,0:T(8,128)(2,1)S(1)}, bf16[48,3072]{1,0:T(8,128)(2,1)S(1)}, u32[]{:S(2)}, u32[]{:S(2)}) collective-permute-start(bf16[48,3072]{1,0:T(8,128)(2,1)S(1)} %collective-permute-done.refs_20_), channel_id=1, source_target_pairs={{0,1},{1,2},{2,3},{3,4},{4,5},{5,6},{6,7},{7,0},{8,9},{9,10},{10,1... | collective-permute-start | bytes 884744 | tf_op jit(solution)/shard_map/ppermute | solution.py:241
  16.4 7.1 %copy-start.4 = (bf16[48,3072]{1,0:T(8,128)(2,1)}, bf16[48,3072]{1,0:T(8,128)(2,1)S(1)}, u32[]{:S(2)}) copy-start(bf16[48,3072]{1,0:T(8,128)(2,1)S(1)} %collective-permute-done.4.refs_9_) | copy-start | bytes 884740
  16.4 7.7 %collective-permute-start.5 = (bf16[48,3072]{1,0:T(8,128)(2,1)S(1)}, bf16[48,3072]{1,0:T(8,128)(2,1)S(1)}, u32[]{:S(2)}, u32[]{:S(2)}) collective-permute-start(bf16[48,3072]{1,0:T(8,128)(2,1)S(1)} %collective-permute-done.4.refs_9_), channel_id=1, source_target_pairs={{0,7},{1,0},{2,1},{3,2},{4,3},{5,4},{6,5},{7,6},{8,15},{9,8},{10,9... | collective-permute-start | bytes 884744 | tf_op jit(solution)/shard_map/ppermute | solution.py:241
  19.5 4.2 %copy-start.5 = (bf16[48,3072]{1,0:T(8,128)(2,1)}, bf16[48,3072]{1,0:T(8,128)(2,1)S(1)}, u32[]{:S(2)}) copy-start(bf16[48,3072]{1,0:T(8,128)(2,1)S(1)} %collective-permute-done.8.refs_21_) | copy-start | bytes 884740
  19.5 20.1 %collective-permute-start.9 = (bf16[48,3072]{1,0:T(8,128)(2,1)S(1)}, bf16[48,3072]{1,0:T(8,128)(2,1)S(1)}, u32[]{:S(2)}, u32[]{:S(2)}) collective-permute-start(bf16[48,3072]{1,0:T(8,128)(2,1)S(1)} %collective-permute-done.8.refs_21_), channel_id=1, source_target_pairs={{0,1},{1,2},{2,3},{3,4},{4,5},{5,6},{6,7},{7,0},{8,9},{9,10},{10,1... | collective-permute-start | bytes 884744 | tf_op jit(solution)/shard_map/ppermute | solution.py:241
  19.5 19.7 %copy-start.7 = (bf16[48,3072]{1,0:T(8,128)(2,1)}, bf16[48,3072]{1,0:T(8,128)(2,1)S(1)}, u32[]{:S(2)}) copy-start(bf16[48,3072]{1,0:T(8,128)(2,1)S(1)} %collective-permute-done.11.refs_8_) | copy-start | bytes 884740
  19.5 20.4 %collective-permute-start.12 = (bf16[48,3072]{1,0:T(8,128)(2,1)S(1)}, bf16[48,3072]{1,0:T(8,128)(2,1)S(1)}, u32[]{:S(2)}, u32[]{:S(2)}) collective-permute-start(bf16[48,3072]{1,0:T(8,128)(2,1)S(1)} %collective-permute-done.11.refs_8_), channel_id=1, source_target_pairs={{0,7},{1,0},{2,1},{3,2},{4,3},{5,4},{6,5},{7,6},{8,15},{9,8},{10,9... | collective-permute-start | bytes 884744 | tf_op jit(solution)/shard_map/ppermute | solution.py:241
  23.5 4.2 %copy-start.8 = (bf16[48,3072]{1,0:T(8,128)(2,1)}, bf16[48,3072]{1,0:T(8,128)(2,1)S(1)}, u32[]{:S(2)}) copy-start(bf16[48,3072]{1,0:T(8,128)(2,1)S(1)} %collective-permute-done.1.refs_18_) | copy-start | bytes 884740
  23.5 10.9 %collective-permute-start.2 = (bf16[48,3072]{1,0:T(8,128)(2,1)S(1)}, bf16[48,3072]{1,0:T(8,128)(2,1)S(1)}, u32[]{:S(2)}, u32[]{:S(2)}) collective-permute-start(bf16[48,3072]{1,0:T(8,128)(2,1)S(1)} %collective-permute-done.1.refs_18_), channel_id=1, source_target_pairs={{0,1},{1,2},{2,3},{3,4},{4,5},{5,6},{6,7},{7,0},{8,9},{9,10},{10,1... | collective-permute-start | bytes 884744 | tf_op jit(solution)/shard_map/ppermute | solution.py:241
  24.1 10.7 %copy-start.9 = (bf16[48,3072]{1,0:T(8,128)(2,1)}, bf16[48,3072]{1,0:T(8,128)(2,1)S(1)}, u32[]{:S(2)}) copy-start(bf16[48,3072]{1,0:T(8,128)(2,1)S(1)} %collective-permute-done.5.refs_11_) | copy-start | bytes 884740
  24.1 11.8 %collective-permute-start.6 = (bf16[48,3072]{1,0:T(8,128)(2,1)S(1)}, bf16[48,3072]{1,0:T(8,128)(2,1)S(1)}, u32[]{:S(2)}, u32[]{:S(2)}) collective-permute-start(bf16[48,3072]{1,0:T(8,128)(2,1)S(1)} %collective-permute-done.5.refs_11_), channel_id=1, source_target_pairs={{0,7},{1,0},{2,1},{3,2},{4,3},{5,4},{6,5},{7,6},{8,15},{9,8},{10,9... | collective-permute-start | bytes 884744 | tf_op jit(solution)/shard_map/ppermute | solution.py:241
  34.4 10.8 %copy-start.12 = (bf16[48,3072]{1,0:T(8,128)(2,1)}, bf16[48,3072]{1,0:T(8,128)(2,1)S(1)}, u32[]{:S(2)}) copy-start(bf16[48,3072]{1,0:T(8,128)(2,1)S(1)} %collective-permute-done.2.refs_16_) | copy-start | bytes 884740
  34.4 8.1 %collective-permute-start.3 = (bf16[48,3072]{1,0:T(8,128)(2,1)S(1)}, bf16[48,3072]{1,0:T(8,128)(2,1)S(1)}, u32[]{:S(2)}, u32[]{:S(2)}) collective-permute-start(bf16[48,3072]{1,0:T(8,128)(2,1)S(1)} %collective-permute-done.2.refs_16_), channel_id=1, source_target_pairs={{0,1},{1,2},{2,3},{3,4},{4,5},{5,6},{6,7},{7,0},{8,9},{9,10},{10,1... | collective-permute-start | bytes 884744 | tf_op jit(solution)/shard_map/ppermute | solution.py:241
  35.9 15.9 %copy-start.13 = (bf16[48,3072]{1,0:T(8,128)(2,1)}, bf16[48,3072]{1,0:T(8,128)(2,1)S(1)}, u32[]{:S(2)}) copy-start(bf16[48,3072]{1,0:T(8,128)(2,1)S(1)} %collective-permute-done.6.refs_13_) | copy-start | bytes 884740
  35.9 9.0 %collective-permute-start.7 = (bf16[48,3072]{1,0:T(8,128)(2,1)S(1)}, bf16[48,3072]{1,0:T(8,128)(2,1)S(1)}, u32[]{:S(2)}, u32[]{:S(2)}) collective-permute-start(bf16[48,3072]{1,0:T(8,128)(2,1)S(1)} %collective-permute-done.6.refs_13_), channel_id=1, source_target_pairs={{0,7},{1,0},{2,1},{3,2},{4,3},{5,4},{6,5},{7,6},{8,15},{9,8},{10,9... | collective-permute-start | bytes 884744 | tf_op jit(solution)/shard_map/ppermute | solution.py:241
  39.5 10.9 %copy-start.10 = (bf16[48,3072]{1,0:T(8,128)(2,1)}, bf16[48,3072]{1,0:T(8,128)(2,1)S(1)}, u32[]{:S(2)}) copy-start(bf16[48,3072]{1,0:T(8,128)(2,1)S(1)} %collective-permute-done.9.refs_19_) | copy-start | bytes 884740
  39.6 10.5 %collective-permute-start.10 = (bf16[48,3072]{1,0:T(8,128)(2,1)S(1)}, bf16[48,3072]{1,0:T(8,128)(2,1)S(1)}, u32[]{:S(2)}, u32[]{:S(2)}) collective-permute-start(bf16[48,3072]{1,0:T(8,128)(2,1)S(1)} %collective-permute-done.9.refs_19_), channel_id=1, source_target_pairs={{0,1},{1,2},{2,3},{3,4},{4,5},{5,6},{6,7},{7,0},{8,9},{9,10},{10,1... | collective-permute-start | bytes 884744 | tf_op jit(solution)/shard_map/ppermute | solution.py:241
  39.9 11.1 %copy-start.11 = (bf16[48,3072]{1,0:T(8,128)(2,1)}, bf16[48,3072]{1,0:T(8,128)(2,1)S(1)}, u32[]{:S(2)}) copy-start(bf16[48,3072]{1,0:T(8,128)(2,1)S(1)} %collective-permute-done.12.refs_10_) | copy-start | bytes 884740
  39.9 11.5 %collective-permute-start.13 = (bf16[48,3072]{1,0:T(8,128)(2,1)S(1)}, bf16[48,3072]{1,0:T(8,128)(2,1)S(1)}, u32[]{:S(2)}, u32[]{:S(2)}) collective-permute-start(bf16[48,3072]{1,0:T(8,128)(2,1)S(1)} %collective-permute-done.12.refs_10_), channel_id=1, source_target_pairs={{0,7},{1,0},{2,1},{3,2},{4,3},{5,4},{6,5},{7,6},{8,15},{9,8},{10,9... | collective-permute-start | bytes 884744 | tf_op jit(solution)/shard_map/ppermute | solution.py:241
  42.5 2.7 %copy-start.14 = (bf16[48,3072]{1,0:T(8,128)(2,1)}, bf16[48,3072]{1,0:T(8,128)(2,1)S(1)}, u32[]{:S(2)}) copy-start(bf16[48,3072]{1,0:T(8,128)(2,1)S(1)} %collective-permute-done.3.refs_14_) | copy-start | bytes 884740
  44.8 0.8 copy-start.15
  50.1 0.8 copy-start.16
  51.4 0.8 copy-start.17
  52.3 19.6 %collective-permute-start.14 = (f32[64,768]{0,1:T(8,128)S(1)}, f32[64,768]{0,1:T(8,128)S(1)}, u32[]{:S(2)}, u32[]{:S(2)}) collective-permute-start(f32[64,768]{0,1:T(8,128)S(1)} %constant_dynamic-slice_fusion), channel_id=1, source_target_pairs={{0,8},{8,0},{1,9},{9,1},{2,10},{10,2},{3,11},{11,3},{4,12},{12,4},... | collective-permute-start | bytes 589832 | tf_op jit(solution)/shard_map/ppermute | solution.py:276
  73.4 23.3 %all-to-all-start = ((bf16[8,48,768]{2,1,0:T(8,128)(2,1)}), bf16[8,48,768]{2,1,0:T(8,128)(2,1)S(1)}, u32[]{:S(2)}, u32[]{:S(2)}) async-start(bf16[8,48,768]{2,1,0:T(8,128)(2,1)} %broadcast_in_dim.29), calls=%async_computation | async-start | bytes 1179648 | tf_op jit(solution)/shard_map/all_to_all | solution.py:251
  113.9 3.7 %copy-start.1 = (bf16[8,48,512]{2,1,0:T(8,128)(2,1)}, bf16[8,48,512]{2,1,0:T(8,128)(2,1)S(1)}, u32[]{:S(2)}) copy-start(bf16[8,48,512]{2,1,0:T(8,128)(2,1)S(1)} %all_to_all.10.refs_2_) | copy-start | bytes 1179652
  113.9 3.7 %collective-permute-start.15 = (bf16[8,48,512]{2,1,0:T(8,128)(2,1)S(1)}, bf16[8,48,512]{2,1,0:T(8,128)(2,1)S(1)}, u32[]{:S(2)}, u32[]{:S(2)}) collective-permute-start(bf16[8,48,512]{2,1,0:T(8,128)(2,1)S(1)} %all_to_all.10.refs_2_), channel_id=1, source_target_pairs={{0,8},{8,0},{1,9},{9,1},{2,10},{10,2},{3,11},{11,3},{4,12},{12,4},... | collective-permute-start | bytes 1179656 | tf_op jit(solution)/shard_map/ppermute | solution.py:293
  116.0 1.6 %copy-start.19 = (f32[16,768]{1,0:T(8,128)}, f32[16,768]{1,0:T(8,128)S(1)}, u32[]{:S(2)}) copy-start(f32[16,768]{1,0:T(8,128)S(1)} %pad_maximum_fusion.1.refs_4_) | copy-start | bytes 147460
  116.1 1.6 %collective-permute-start.16 = (f32[16,768]{1,0:T(8,128)S(1)}, f32[16,768]{1,0:T(8,128)S(1)}, u32[]{:S(2)}, u32[]{:S(2)}) collective-permute-start(f32[16,768]{1,0:T(8,128)S(1)} %pad_maximum_fusion.1.refs_4_), channel_id=1, source_target_pairs={{0,8},{8,0},{1,9},{9,1},{2,10},{10,2},{3,11},{11,3},{4,12},{12,4},... | collective-permute-start | bytes 147464 | tf_op jit(solution)/shard_map/ppermute | solution.py:297
  117.6 0.6 copy-start.21
  117.6 0.8 copy-start.18

commit v4 on v3

--- a/solution.py
+++ b/solution.py
@@ -11,6 +11,7 @@
 SUB = 8
 BLK = 128
 TILE = 512
+NEAR = 2
 
 
 def split(a):
@@ -39,6 +40,11 @@
         odd = [terms[-1]] if len(terms) % 2 else []
         terms = [a + b for a, b in zip(terms[::2], terms[1::2])] + odd
     return terms[0]
+
+
+def around(x, before, after):
+    parts = [jnp.zeros((before, x.shape[1]), x.dtype), x, jnp.zeros((after, x.shape[1]), x.dtype)]
+    return jnp.concatenate([part for part in parts if part.shape[0]], axis=0)
 
 
 def inverse_of_factor(rows, inv):
@@ -77,12 +83,26 @@
             ahead[m] - total_of([lower[j] * wide(scaled[j][m : m + 1]) for j in range(SUB)])
             for m in range(SUB)
         ]
+        far = min(p + 1 + NEAR, len(rows))
+        if far < len(rows):
+            pivots = jnp.concatenate([v, g], axis=1)
+            zeros = jnp.zeros_like(pivots)
+            pivots = [zeros, pivots] if p % 2 else [pivots, zeros]
+            pivots = split(jnp.concatenate(pivots, axis=0))
+            first = p // 2 * 2 * SUB
+            pivots = [around(x, first, BLK - first - 2 * SUB) for x in pivots]
+            taken = dot3(split(jnp.concatenate(rows[far:], axis=0)), pivots, ((1,), (0,)))
         vs = [wide(v[j : j + 1]) for j in range(SUB)]
         gs = [wide(g[j : j + 1]) for j in range(SUB)]
         for q in range(p + 1, len(rows)):
-            c = below if q == p + 1 else lanes(rows[q], k)
-            rows[q] = rows[q] - total_of([c[j] * vs[j] for j in range(SUB)])
-            inv[q] = inv[q] - total_of([c[j] * gs[j] for j in range(SUB)])
+            if q < far:
+                c = below if q == p + 1 else lanes(rows[q], k)
+                rows[q] = rows[q] - total_of([c[j] * vs[j] for j in range(SUB)])
+                inv[q] = inv[q] - total_of([c[j] * gs[j] for j in range(SUB)])
+            else:
+                i = (q - far) * SUB
+                rows[q] = rows[q] - taken[i : i + SUB, :BLK]
+                inv[q] = inv[q] - taken[i : i + SUB, BLK:]
     return inv
 
 
@@ -142,12 +162,15 @@
     far = count // 2
     used = (far + 1) * own
     lane = lax.broadcasted_iota(jnp.int32, (half, mine_ref.shape[2]), 1)
+    twice = (lane < own) | (lane >= far * own)
+    weight = jnp.where(lane < used, jnp.where(twice, 0.5, 1.0), 0.0)
     pad = jnp.zeros((half, n - mine_ref.shape[2]), jnp.float32)
     for x in range(count):
         for h in range(2):
             mine, other = mine_ref[x].astype(jnp.float32), other_ref[x].astype(jnp.float32)
             rows = jnp.where(core == h, mine, other)
-            rows = jnp.concatenate([jnp.where(lane < used, rows, 0.0), pad], axis=1)
+            rows = jnp.where(lane < used, rows, 0.0) * weight
+            rows = jnp.concatenate([rows, pad], axis=1)
             shift = ((x - far) * own) % n
             if shift:
                 rows = pltpu.roll(rows, shift, 1)
@@ -176,15 +199,13 @@
     coupling = dot3(split(overlap), inverse, ((1,), (1,)))
     applied = -dot3(split(coupling), inverse, ((1,), (0,)))
     own_rows = a_ref[pl.ds(pl.multiple_of(band * own, SUB), own), :]
-    hi, lo = split(jnp.concatenate([own_rows, applied], axis=0))
-    both = jnp.concatenate([hi, lo], axis=0)
+    coefs = jnp.concatenate([own_rows, applied], axis=0).astype(jnp.bfloat16)
 
     for copy in copies:
         copy.wait()
-    rows = hi.shape[0]
     for at in range(0, w_ref.shape[1], TILE):
-        out = jnp.dot(both, w_ref[:, at : at + TILE], preferred_element_type=jnp.float32)
-        out = (out[:rows] + out[rows:]).astype(jnp.bfloat16)
+        out = jnp.dot(coefs, w_ref[:, at : at + TILE], preferred_element_type=jnp.float32)
+        out = out.astype(jnp.bfloat16)
         p_ref[:, at : at + TILE] = out[:own]
         x_ref[:, at : at + TILE] = out[own:]
 
@@ -228,21 +249,29 @@
             left, piece, (((1,), (1,)), ((), ())), preferred_element_type=jnp.float32
         )
 
-    got, parts = {(0, h): halves[h] for h in range(2)}, {}
-    moving = {(way, h): halves[h] for way, h in ((1, 0), (-1, 1), (1, 1), (-1, 0))}
-    fresh = list(got)
+    longer = ((1, 0), (-1, 1))
+    got = {(0, h): halves[h] for h in range(2)}
+    parts = {key: dot(x) for key, x in got.items()}
+    moving = {(way, h): halves[h] for way, h in longer + ((1, 1), (-1, 0))}
     for s in range(1, far + 1):
-        if s == far:
-            moving = {key: moving[key] for key in ((1, 0), (-1, 1))}
-        for way, h in list(moving):
-            x, before = moving[way, h], (-way * (s - 2) % count, h)
-            if s > 1:
+        fresh = {}
+        for (way, h), x in moving.items():
+            long = (way, h) in longer
+            if s == far and not long:
+                continue
+            before = (-way * (s - 2) % count, h) if s > 1 else (0, h)
+            if s > 1 or not long:
                 x, parts[before] = lax.optimization_barrier((x, parts[before]))
-            moving[way, h] = lax.ppermute(x, "band", ways[way])
-        parts.update({key: dot(got[key]) for key in fresh})
-        fresh = [(-way * s % count, h) for way, h in moving]
-        got.update(zip(fresh, moving.values()))
-    parts.update({key: dot(got[key]) for key in fresh})
+            fresh[way, h] = lax.ppermute(x, "band", ways[way])
+        if s > 1:
+            for way, h in moving:
+                key = (-way * (s - 1) % count, h)
+                parts[key] = dot(got[key])
+        moving = fresh
+        got.update({(-way * s % count, h): x for (way, h), x in moving.items()})
+    for way, h in moving:
+        key = (-way * far % count, h)
+        parts[key] = dot(got[key])
     return got, parts
 
 
@@ -286,10 +315,7 @@
         axis=1,
     )
     summed = to_all(packed.astype(jnp.bfloat16), "y").astype(jnp.float32).sum(axis=0) / total
-    column = lax.broadcasted_iota(jnp.int32, (ho, used), 1)
-    twice = (column < own) | ((column >= far * own) & (column < (far + 1) * own))
-    half_margin = -summed[:, :used] * jnp.where(twice, 0.5, 1.0)
-    margin = to_all(half_margin.astype(jnp.bfloat16), "band")
+    margin = to_all((-summed[:, :used]).astype(jnp.bfloat16), "band")
     other_margin = lax.ppermute(margin, "core", swap)
     overlap = jnp.concatenate(
         [summed[i * hb : (i + 1) * hb, used:] for i in range(fold)], axis=1

time: 150 us -> 144 us (0.960)
  waiting for transfers between devices: 42.4 us -> 17 us
  blocking collectives: 17 us -> 41.1 us
  Pallas kernels: 31.5 us -> 28.4 us
  starting transfers between devices: 47.8 us -> 45 us
    all_to_all x1 -> x2, blocking collectives: 17 us -> 41.1 us  [to_all(): lax.all_to_all(jnp.broadcast_to(shard[None], (count, *shard.shape)), axis...]
    all_to_all x1 -> x0, waiting for transfers between devices: 19.4 us -> none  [to_all(): lax.all_to_all(jnp.broadcast_to(shard[None], (count, *shard.shape)), axis...]
    ppermute x14, waiting for transfers between devices: 20.5 us -> 14.4 us  [ring(): fresh[way, h] = lax.ppermute(x, 'band', ways[way])]
    all_to_all x1 -> x0, starting transfers between devices: 3.95 us -> none  [to_all(): lax.all_to_all(jnp.broadcast_to(shard[None], (count, *shard.shape)), axis...]
    pallas_call x1, Pallas kernels: 31.5 us -> 28.4 us  [project(): pl.pallas_call(functools.partial(project_kernel, count), out_shape=[jax.S...]
  transfers between devices with their start and end apart: 18 -> 17, of which waited for: 8 -> 8; matrix products, arithmetic and copies ran while one was open for 3% -> 4% of each run, Pallas kernels for 0% -> 0%
where the time goes in v4:
time: 144 us; the launch traced here: 143 us
  starting transfers between devices  45 us (31%)
  blocking collectives  41.1 us (29%)
  Pallas kernels  28.4 us (20%)
  waiting for transfers between devices  17 us (12%)
  matrix products  7.01 us (5%)
  local copies, waits for them, and re-layouts  2.01 us (1%)
  other arithmetic  1.55 us (1%)
    all_to_all x2, blocking collectives, to_all(): lax.all_to_all(jnp.broadcast_to(shard[None], (count, *shard.shape)), axis...  41.1 us
    pallas_call x1, Pallas kernels, project(): pl.pallas_call(functools.partial(project_kernel, count), out_shape=[jax.S...  28.4 us
    ppermute x14, starting transfers between devices, ring(): fresh[way, h] = lax.ppermute(x, 'band', ways[way])  24.4 us
    ppermute x1, starting transfers between devices, shards(): kept = kept + lax.ppermute(sent, 'core', swap)  17.5 us
    ppermute x14, waiting for transfers between devices, ring(): fresh[way, h] = lax.ppermute(x, 'band', ways[way])  14.4 us
    dot_general x16, matrix products, dot(): lax.dot_general(left, piece, (((1,), (1,)), ((), ())), preferred_element_...  7.01 us
    ppermute x1, starting transfers between devices, shards(): other_margin = lax.ppermute(margin, 'core', swap)  3.02 us
  transfers between devices with their start and end apart: 17, of which 8 were waited for; matrix products, arithmetic and copies ran while one was open for 4% of the time, Pallas kernels for 0%

profile of v4, /device:TPU:513, one launch (start us, length us, event | category | flops | bytes accessed | tf_op | source)
XLA Modules:
  0.0 143.5 jit_solution(12132256058766878459)
XLA Ops:
  0.6 1.2 negate_convert_fusion
  1.9 2.3 %collective-permute-start = (bf16[48,3072]{1,0:T(8,128)(2,1)S(1)}, bf16[48,3072]{1,0:T(8,128)(2,1)S(1)}, u32[]{:S(2)}, u32[]{:S(2)}) collective-permute-start(bf16[48,3072]{1,0:T(8,128)(2,1)S(1)} %get-tuple-element.41.refs_6_), channel_id=1, source_target_pairs={{0,1},{1,2},{2,3},{3,4},{4,5},{5,6},{6,7},{7,0},{8,9},{9,10},{10,1... | collective-permute-start | bytes 884744 | tf_op jit(solution)/shard_map/ppermute | solution.py:265
  4.2 2.3 %collective-permute-start.4 = (bf16[48,3072]{1,0:T(8,128)(2,1)S(1)}, bf16[48,3072]{1,0:T(8,128)(2,1)S(1)}, u32[]{:S(2)}, u32[]{:S(2)}) collective-permute-start(bf16[48,3072]{1,0:T(8,128)(2,1)S(1)} %get-tuple-element.34.refs_7_), channel_id=1, source_target_pairs={{0,7},{1,0},{2,1},{3,2},{4,3},{5,4},{6,5},{7,6},{8,15},{9,8},{10,9... | collective-permute-start | bytes 884744 | tf_op jit(solution)/shard_map/ppermute | solution.py:265
  6.6 0.1 pad_maximum_fusion
  6.7 1.0 fusion.1
  7.7 1.0 fusion.3
  8.7 2.7 %collective-permute-start.11 = (bf16[48,3072]{1,0:T(8,128)(2,1)S(1)}, bf16[48,3072]{1,0:T(8,128)(2,1)S(1)}, u32[]{:S(2)}, u32[]{:S(2)}) collective-permute-start(bf16[48,3072]{1,0:T(8,128)(2,1)S(1)} %get-tuple-element.41.refs_6_), channel_id=1, source_target_pairs={{0,7},{1,0},{2,1},{3,2},{4,3},{5,4},{6,5},{7,6},{8,15},{9,8},{10,9... | collective-permute-start | bytes 884744 | tf_op jit(solution)/shard_map/ppermute | solution.py:265
  11.4 0.1 collective-permute-start.1
  11.4 3.1 %collective-permute-start.5 = (bf16[48,3072]{1,0:T(8,128)(2,1)S(1)}, bf16[48,3072]{1,0:T(8,128)(2,1)S(1)}, u32[]{:S(2)}, u32[]{:S(2)}) collective-permute-start(bf16[48,3072]{1,0:T(8,128)(2,1)S(1)} %collective-permute-done.4.refs_9_), channel_id=1, source_target_pairs={{0,7},{1,0},{2,1},{3,2},{4,3},{5,4},{6,5},{7,6},{8,15},{9,8},{10,9... | collective-permute-start | bytes 884744 | tf_op jit(solution)/shard_map/ppermute | solution.py:265
  14.5 1.1 collective-permute-start.9
  15.7 2.8 %collective-permute-start.12 = (bf16[48,3072]{1,0:T(8,128)(2,1)S(1)}, bf16[48,3072]{1,0:T(8,128)(2,1)S(1)}, u32[]{:S(2)}, u32[]{:S(2)}) collective-permute-start(bf16[48,3072]{1,0:T(8,128)(2,1)S(1)} %collective-permute-done.11.refs_8_), channel_id=1, source_target_pairs={{0,7},{1,0},{2,1},{3,2},{4,3},{5,4},{6,5},{7,6},{8,15},{9,8},{10,9... | collective-permute-start | bytes 884744 | tf_op jit(solution)/shard_map/ppermute | solution.py:265
  18.4 0.4 fusion.10
  18.8 0.4 fusion.12
  19.2 0.0 copy-done.4
  19.2 0.8 collective-permute-start.2
  20.0 0.4 fusion.14
  20.4 0.0 collective-permute-done.5.refs_11_
  20.4 2.9 %collective-permute-start.6 = (bf16[48,3072]{1,0:T(8,128)(2,1)S(1)}, bf16[48,3072]{1,0:T(8,128)(2,1)S(1)}, u32[]{:S(2)}, u32[]{:S(2)}) collective-permute-start(bf16[48,3072]{1,0:T(8,128)(2,1)S(1)} %collective-permute-done.5.refs_11_), channel_id=1, source_target_pairs={{0,7},{1,0},{2,1},{3,2},{4,3},{5,4},{6,5},{7,6},{8,15},{9,8},{10,9... | collective-permute-start | bytes 884744 | tf_op jit(solution)/shard_map/ppermute | solution.py:265
  23.3 0.4 fusion.11
  23.7 0.0 copy-done.8
  23.7 3.8 %collective-permute-done.2.refs_16_ = bf16[48,3072]{1,0:T(8,128)(2,1)S(1)} collective-permute-done((bf16[48,3072]{1,0:T(8,128)(2,1)S(1)}, bf16[48,3072]{1,0:T(8,128)(2,1)S(1)}, u32[]{:S(2)}, u32[]{:S(2)}) %collective-permute-start.2) | collective-permute-done | bytes 294944 | tf_op jit(solution)/shard_map/ppermute | solution.py:265
  27.5 0.2 collective-permute-start.3
  27.7 0.4 fusion.13
  28.1 0.0 copy-done.9
  28.1 2.6 %collective-permute-done.6.refs_13_ = bf16[48,3072]{1,0:T(8,128)(2,1)S(1)} collective-permute-done((bf16[48,3072]{1,0:T(8,128)(2,1)S(1)}, bf16[48,3072]{1,0:T(8,128)(2,1)S(1)}, u32[]{:S(2)}, u32[]{:S(2)}) %collective-permute-start.6) | collective-permute-done | bytes 294944 | tf_op jit(solution)/shard_map/ppermute | solution.py:265
  30.7 2.3 %collective-permute-start.7 = (bf16[48,3072]{1,0:T(8,128)(2,1)S(1)}, bf16[48,3072]{1,0:T(8,128)(2,1)S(1)}, u32[]{:S(2)}, u32[]{:S(2)}) collective-permute-start(bf16[48,3072]{1,0:T(8,128)(2,1)S(1)} %collective-permute-done.6.refs_13_), channel_id=1, source_target_pairs={{0,7},{1,0},{2,1},{3,2},{4,3},{5,4},{6,5},{7,6},{8,15},{9,8},{10,9... | collective-permute-start | bytes 884744 | tf_op jit(solution)/shard_map/ppermute | solution.py:265
  33.0 0.4 fusion.15
  33.4 0.0 collective-permute-done.9.refs_19_
  33.4 3.3 %collective-permute-start.10 = (bf16[48,3072]{1,0:T(8,128)(2,1)S(1)}, bf16[48,3072]{1,0:T(8,128)(2,1)S(1)}, u32[]{:S(2)}, u32[]{:S(2)}) collective-permute-start(bf16[48,3072]{1,0:T(8,128)(2,1)S(1)} %collective-permute-done.9.refs_19_), channel_id=1, source_target_pairs={{0,1},{1,2},{2,3},{3,4},{4,5},{5,6},{6,7},{7,0},{8,9},{9,10},{10,1... | collective-permute-start | bytes 884744 | tf_op jit(solution)/shard_map/ppermute | solution.py:265
  36.7 0.6 collective-permute-start.13
  37.2 0.7 collective-permute-done.3.refs_14_
  37.9 0.4 convolution_dynamic-update-slice_fusion.7
  38.3 3.4 %collective-permute-done.7.refs_15_ = bf16[48,3072]{1,0:T(8,128)(2,1)S(1)} collective-permute-done((bf16[48,3072]{1,0:T(8,128)(2,1)S(1)}, bf16[48,3072]{1,0:T(8,128)(2,1)S(1)}, u32[]{:S(2)}, u32[]{:S(2)}) %collective-permute-start.7) | collective-permute-done | bytes 294944 | tf_op jit(solution)/shard_map/ppermute | solution.py:265
  41.7 0.4 convolution_dynamic-update-slice_fusion.6
  42.1 0.4 convolution_dynamic-update-slice_fusion.5
  42.5 2.2 %collective-permute-done.10.refs_17_ = bf16[48,3072]{1,0:T(8,128)(2,1)S(1)} collective-permute-done((bf16[48,3072]{1,0:T(8,128)(2,1)S(1)}, bf16[48,3072]{1,0:T(8,128)(2,1)S(1)}, u32[]{:S(2)}, u32[]{:S(2)}) %collective-permute-start.10) | collective-permute-done | bytes 294944 | tf_op jit(solution)/shard_map/ppermute | solution.py:265
  44.7 0.4 convolution_dynamic-update-slice_fusion.4
  45.0 0.0 copy-start.22
  45.1 0.4 convolution_dynamic-update-slice_fusion.3
  45.5 0.3 copy-done.22
  45.8 0.0 copy-done.21
  45.8 0.4 convolution_dynamic-update-slice_fusion.2
  46.2 1.8 %collective-permute-done.13.refs_12_ = bf16[48,3072]{1,0:T(8,128)(2,1)S(1)} collective-permute-done((bf16[48,3072]{1,0:T(8,128)(2,1)S(1)}, bf16[48,3072]{1,0:T(8,128)(2,1)S(1)}, u32[]{:S(2)}, u32[]{:S(2)}) %collective-permute-start.13) | collective-permute-done | bytes 294944 | tf_op jit(solution)/shard_map/ppermute | solution.py:265
  48.0 0.4 convolution_dynamic-update-slice_fusion.1
  48.4 0.0 copy-done.13
  48.4 0.4 convolution_dynamic-update-slice_fusion
  48.8 0.2 constant_dynamic-slice_fusion
  48.9 17.5 %collective-permute-start.14 = (f32[64,768]{0,1:T(8,128)S(1)}, f32[64,768]{0,1:T(8,128)S(1)}, u32[]{:S(2)}, u32[]{:S(2)}) collective-permute-start(f32[64,768]{0,1:T(8,128)S(1)} %constant_dynamic-slice_fusion), channel_id=1, source_target_pairs={{0,8},{8,0},{1,9},{9,1},{2,10},{10,2},{3,11},{11,3},{4,12},{12,4},... | collective-permute-start | bytes 589832 | tf_op jit(solution)/shard_map/ppermute | solution.py:305
  66.4 1.3 collective-permute-done.14
  67.8 0.2 add_convert_fusion
  67.9 0.1 fusion.7
  68.1 0.1 copy.10
  68.2 0.1 copy.11
  68.2 0.1 copy.12
  68.3 0.1 copy.13
  68.5 22.7 %all_to_all.10 = bf16[8,48,768]{2,1,0:T(8,128)(2,1)S(1)} all-to-all(bf16[8,48,768]{2,1,0:T(8,128)(2,1)S(1)} %broadcast_in_dim.10), channel_id=1, replica_groups=mesh['img'=2,'y'=8,'core'=2,'band'=8] {'y'}, dimensions={0} | all-to-all | bytes 1179648 | tf_op jit(solution)/shard_map/all_to_all | solution.py:280
  91.3 0.1 convert_reduce_fusion
  91.4 18.3 %all_to_all.11.refs_2_ = bf16[8,48,512]{2,1,0:T(8,128)(2,1)S(1)} all-to-all(bf16[8,48,512]{2,1,0:T(8,128)(2,1)S(1)} %broadcast_in_dim.22), channel_id=1, replica_groups=mesh['img'=2,'y'=8,'core'=2,'band'=8] {'band'}, dimensions={0} | all-to-all | bytes 786432 | tf_op jit(solution)/shard_map/all_to_all | solution.py:280
  109.7 3.0 %collective-permute-start.15 = (bf16[8,48,512]{2,1,0:T(8,128)(2,1)S(1)}, bf16[8,48,512]{2,1,0:T(8,128)(2,1)S(1)}, u32[]{:S(2)}, u32[]{:S(2)}) collective-permute-start(bf16[8,48,512]{2,1,0:T(8,128)(2,1)S(1)} %all_to_all.11.refs_2_), channel_id=1, source_target_pairs={{0,8},{8,0},{1,9},{9,1},{2,10},{10,2},{3,11},{11,3},{4,12},{12,4},... | collective-permute-start | bytes 1179656 | tf_op jit(solution)/shard_map/ppermute | solution.py:319
  112.8 0.1 collective-permute-start.16
  112.9 1.2 collective-permute-done.16.refs_5_
  114.2 0.6 copy-done.23
  114.8 0.2 copy-done.18
  114.9 28.4 %project.1 = (bf16[96,3072]{1,0:T(8,128)(2,1)}, bf16[32,3072]{1,0:T(8,128)(2,1)}) custom-call(s32[1]{0:T(128)} %bitcast.refs_0_, s32[1]{0:T(128)} %bitcast.1.refs_1_, bf16[8,48,512]{2,1,0:T(8,128)(2,1)} %copy-done.1, bf16[8,48,512]{2,1,0:T(8,128)(2,1)} %copy-done.18, f32[16,768]{1,0:T(8,128)} %copy-done.19, f32[16,768]{1,0:T(8,128)} %copy-done.23, ...), custom_call_target="tpu_custom_call" | custom-call | tf_op jit(solution)/shard_map/project/pallas_call | solution.py:217
  (66 shorter events, 0.4 us)
Async XLA Ops:
  1.8 4.7 %copy-start = (bf16[96,3072]{1,0:T(8,128)(2,1)S(1)}, bf16[96,3072]{1,0:T(8,128)(2,1)}, u32[]{:S(2)}) copy-start(bf16[96,3072]{1,0:T(8,128)(2,1)} %param.3) | copy-start | bytes 1769476
  1.9 5.8 %copy-start.2 = (bf16[48,3072]{1,0:T(8,128)(2,1)}, bf16[48,3072]{1,0:T(8,128)(2,1)S(1)}, u32[]{:S(2)}) copy-start(bf16[48,3072]{1,0:T(8,128)(2,1)S(1)} %get-tuple-element.34.refs_7_) | copy-start | bytes 884740
  1.9 6.8 %copy-start.3 = (bf16[48,3072]{1,0:T(8,128)(2,1)}, bf16[48,3072]{1,0:T(8,128)(2,1)S(1)}, u32[]{:S(2)}) copy-start(bf16[48,3072]{1,0:T(8,128)(2,1)S(1)} %get-tuple-element.41.refs_6_) | copy-start | bytes 884740
  1.9 4.7 %copy-start.20 = (bf16[32,3072]{1,0:T(8,128)(2,1)S(1)}, bf16[32,3072]{1,0:T(8,128)(2,1)}, u32[]{:S(2)}) copy-start(bf16[32,3072]{1,0:T(8,128)(2,1)} %param.5) | copy-start | bytes 589828
  1.9 9.4 %collective-permute-start = (bf16[48,3072]{1,0:T(8,128)(2,1)S(1)}, bf16[48,3072]{1,0:T(8,128)(2,1)S(1)}, u32[]{:S(2)}, u32[]{:S(2)}) collective-permute-start(bf16[48,3072]{1,0:T(8,128)(2,1)S(1)} %get-tuple-element.41.refs_6_), channel_id=1, source_target_pairs={{0,1},{1,2},{2,3},{3,4},{4,5},{5,6},{6,7},{7,0},{8,9},{9,10},{10,1... | collective-permute-start | bytes 884744 | tf_op jit(solution)/shard_map/ppermute | solution.py:265
  4.2 7.2 %collective-permute-start.4 = (bf16[48,3072]{1,0:T(8,128)(2,1)S(1)}, bf16[48,3072]{1,0:T(8,128)(2,1)S(1)}, u32[]{:S(2)}, u32[]{:S(2)}) collective-permute-start(bf16[48,3072]{1,0:T(8,128)(2,1)S(1)} %get-tuple-element.34.refs_7_), channel_id=1, source_target_pairs={{0,7},{1,0},{2,1},{3,2},{4,3},{5,4},{6,5},{7,6},{8,15},{9,8},{10,9... | collective-permute-start | bytes 884744 | tf_op jit(solution)/shard_map/ppermute | solution.py:265
  7.7 6.8 %collective-permute-start.8 = (bf16[48,3072]{1,0:T(8,128)(2,1)S(1)}, bf16[48,3072]{1,0:T(8,128)(2,1)S(1)}, u32[]{:S(2)}, u32[]{:S(2)}) collective-permute-start(bf16[48,3072]{1,0:T(8,128)(2,1)S(1)} %get-tuple-element.34.refs_7_), channel_id=1, source_target_pairs={{0,1},{1,2},{2,3},{3,4},{4,5},{5,6},{6,7},{7,0},{8,9},{9,10},{10,1... | collective-permute-start | bytes 884744 | tf_op jit(solution)/shard_map/ppermute | solution.py:265
  8.7 7.0 %collective-permute-start.11 = (bf16[48,3072]{1,0:T(8,128)(2,1)S(1)}, bf16[48,3072]{1,0:T(8,128)(2,1)S(1)}, u32[]{:S(2)}, u32[]{:S(2)}) collective-permute-start(bf16[48,3072]{1,0:T(8,128)(2,1)S(1)} %get-tuple-element.41.refs_6_), channel_id=1, source_target_pairs={{0,7},{1,0},{2,1},{3,2},{4,3},{5,4},{6,5},{7,6},{8,15},{9,8},{10,9... | collective-permute-start | bytes 884744 | tf_op jit(solution)/shard_map/ppermute | solution.py:265
  11.4 7.8 %copy-start.4 = (bf16[48,3072]{1,0:T(8,128)(2,1)}, bf16[48,3072]{1,0:T(8,128)(2,1)S(1)}, u32[]{:S(2)}) copy-start(bf16[48,3072]{1,0:T(8,128)(2,1)S(1)} %collective-permute-done.refs_20_) | copy-start | bytes 884740
  11.4 7.8 %collective-permute-start.1 = (bf16[48,3072]{1,0:T(8,128)(2,1)S(1)}, bf16[48,3072]{1,0:T(8,128)(2,1)S(1)}, u32[]{:S(2)}, u32[]{:S(2)}) collective-permute-start(bf16[48,3072]{1,0:T(8,128)(2,1)S(1)} %collective-permute-done.refs_20_), channel_id=1, source_target_pairs={{0,1},{1,2},{2,3},{3,4},{4,5},{5,6},{6,7},{7,0},{8,9},{9,10},{10,1... | collective-permute-start | bytes 884744 | tf_op jit(solution)/shard_map/ppermute | solution.py:265
  11.4 7.8 %copy-start.5 = (bf16[48,3072]{1,0:T(8,128)(2,1)}, bf16[48,3072]{1,0:T(8,128)(2,1)S(1)}, u32[]{:S(2)}) copy-start(bf16[48,3072]{1,0:T(8,128)(2,1)S(1)} %collective-permute-done.4.refs_9_) | copy-start | bytes 884740
  11.4 8.9 %collective-permute-start.5 = (bf16[48,3072]{1,0:T(8,128)(2,1)S(1)}, bf16[48,3072]{1,0:T(8,128)(2,1)S(1)}, u32[]{:S(2)}, u32[]{:S(2)}) collective-permute-start(bf16[48,3072]{1,0:T(8,128)(2,1)S(1)} %collective-permute-done.4.refs_9_), channel_id=1, source_target_pairs={{0,7},{1,0},{2,1},{3,2},{4,3},{5,4},{6,5},{7,6},{8,15},{9,8},{10,9... | collective-permute-start | bytes 884744 | tf_op jit(solution)/shard_map/ppermute | solution.py:265
  14.5 5.5 %copy-start.6 = (bf16[48,3072]{1,0:T(8,128)(2,1)}, bf16[48,3072]{1,0:T(8,128)(2,1)S(1)}, u32[]{:S(2)}) copy-start(bf16[48,3072]{1,0:T(8,128)(2,1)S(1)} %collective-permute-done.8.refs_21_) | copy-start | bytes 884740
  14.5 18.9 %collective-permute-start.9 = (bf16[48,3072]{1,0:T(8,128)(2,1)S(1)}, bf16[48,3072]{1,0:T(8,128)(2,1)S(1)}, u32[]{:S(2)}, u32[]{:S(2)}) collective-permute-start(bf16[48,3072]{1,0:T(8,128)(2,1)S(1)} %collective-permute-done.8.refs_21_), channel_id=1, source_target_pairs={{0,1},{1,2},{2,3},{3,4},{4,5},{5,6},{6,7},{7,0},{8,9},{9,10},{10,1... | collective-permute-start | bytes 884744 | tf_op jit(solution)/shard_map/ppermute | solution.py:265
  15.7 17.3 %copy-start.7 = (bf16[48,3072]{1,0:T(8,128)(2,1)}, bf16[48,3072]{1,0:T(8,128)(2,1)S(1)}, u32[]{:S(2)}) copy-start(bf16[48,3072]{1,0:T(8,128)(2,1)S(1)} %collective-permute-done.11.refs_8_) | copy-start | bytes 884740
  15.7 21.0 %collective-permute-start.12 = (bf16[48,3072]{1,0:T(8,128)(2,1)S(1)}, bf16[48,3072]{1,0:T(8,128)(2,1)S(1)}, u32[]{:S(2)}, u32[]{:S(2)}) collective-permute-start(bf16[48,3072]{1,0:T(8,128)(2,1)S(1)} %collective-permute-done.11.refs_8_), channel_id=1, source_target_pairs={{0,7},{1,0},{2,1},{3,2},{4,3},{5,4},{6,5},{7,6},{8,15},{9,8},{10,9... | collective-permute-start | bytes 884744 | tf_op jit(solution)/shard_map/ppermute | solution.py:265
  19.2 4.5 %copy-start.8 = (bf16[48,3072]{1,0:T(8,128)(2,1)}, bf16[48,3072]{1,0:T(8,128)(2,1)S(1)}, u32[]{:S(2)}) copy-start(bf16[48,3072]{1,0:T(8,128)(2,1)S(1)} %collective-permute-done.1.refs_18_) | copy-start | bytes 884740
  19.2 8.3 %collective-permute-start.2 = (bf16[48,3072]{1,0:T(8,128)(2,1)S(1)}, bf16[48,3072]{1,0:T(8,128)(2,1)S(1)}, u32[]{:S(2)}, u32[]{:S(2)}) collective-permute-start(bf16[48,3072]{1,0:T(8,128)(2,1)S(1)} %collective-permute-done.1.refs_18_), channel_id=1, source_target_pairs={{0,1},{1,2},{2,3},{3,4},{4,5},{5,6},{6,7},{7,0},{8,9},{9,10},{10,1... | collective-permute-start | bytes 884744 | tf_op jit(solution)/shard_map/ppermute | solution.py:265
  20.4 7.7 %copy-start.9 = (bf16[48,3072]{1,0:T(8,128)(2,1)}, bf16[48,3072]{1,0:T(8,128)(2,1)S(1)}, u32[]{:S(2)}) copy-start(bf16[48,3072]{1,0:T(8,128)(2,1)S(1)} %collective-permute-done.5.refs_11_) | copy-start | bytes 884740
  20.4 10.3 %collective-permute-start.6 = (bf16[48,3072]{1,0:T(8,128)(2,1)S(1)}, bf16[48,3072]{1,0:T(8,128)(2,1)S(1)}, u32[]{:S(2)}, u32[]{:S(2)}) collective-permute-start(bf16[48,3072]{1,0:T(8,128)(2,1)S(1)} %collective-permute-done.5.refs_11_), channel_id=1, source_target_pairs={{0,7},{1,0},{2,1},{3,2},{4,3},{5,4},{6,5},{7,6},{8,15},{9,8},{10,9... | collective-permute-start | bytes 884744 | tf_op jit(solution)/shard_map/ppermute | solution.py:265
  27.5 14.6 %copy-start.12 = (bf16[48,3072]{1,0:T(8,128)(2,1)}, bf16[48,3072]{1,0:T(8,128)(2,1)S(1)}, u32[]{:S(2)}) copy-start(bf16[48,3072]{1,0:T(8,128)(2,1)S(1)} %collective-permute-done.2.refs_16_) | copy-start | bytes 884740
  27.5 10.4 %collective-permute-start.3 = (bf16[48,3072]{1,0:T(8,128)(2,1)S(1)}, bf16[48,3072]{1,0:T(8,128)(2,1)S(1)}, u32[]{:S(2)}, u32[]{:S(2)}) collective-permute-start(bf16[48,3072]{1,0:T(8,128)(2,1)S(1)} %collective-permute-done.2.refs_16_), channel_id=1, source_target_pairs={{0,1},{1,2},{2,3},{3,4},{4,5},{5,6},{6,7},{7,0},{8,9},{9,10},{10,1... | collective-permute-start | bytes 884744 | tf_op jit(solution)/shard_map/ppermute | solution.py:265
  30.7 17.7 %copy-start.13 = (bf16[48,3072]{1,0:T(8,128)(2,1)}, bf16[48,3072]{1,0:T(8,128)(2,1)S(1)}, u32[]{:S(2)}) copy-start(bf16[48,3072]{1,0:T(8,128)(2,1)S(1)} %collective-permute-done.6.refs_13_) | copy-start | bytes 884740
  30.7 11.0 %collective-permute-start.7 = (bf16[48,3072]{1,0:T(8,128)(2,1)S(1)}, bf16[48,3072]{1,0:T(8,128)(2,1)S(1)}, u32[]{:S(2)}, u32[]{:S(2)}) collective-permute-start(bf16[48,3072]{1,0:T(8,128)(2,1)S(1)} %collective-permute-done.6.refs_13_), channel_id=1, source_target_pairs={{0,7},{1,0},{2,1},{3,2},{4,3},{5,4},{6,5},{7,6},{8,15},{9,8},{10,9... | collective-permute-start | bytes 884744 | tf_op jit(solution)/shard_map/ppermute | solution.py:265
  33.4 11.7 %copy-start.10 = (bf16[48,3072]{1,0:T(8,128)(2,1)}, bf16[48,3072]{1,0:T(8,128)(2,1)S(1)}, u32[]{:S(2)}) copy-start(bf16[48,3072]{1,0:T(8,128)(2,1)S(1)} %collective-permute-done.9.refs_19_) | copy-start | bytes 884740
  33.4 11.3 %collective-permute-start.10 = (bf16[48,3072]{1,0:T(8,128)(2,1)S(1)}, bf16[48,3072]{1,0:T(8,128)(2,1)S(1)}, u32[]{:S(2)}, u32[]{:S(2)}) collective-permute-start(bf16[48,3072]{1,0:T(8,128)(2,1)S(1)} %collective-permute-done.9.refs_19_), channel_id=1, source_target_pairs={{0,1},{1,2},{2,3},{3,4},{4,5},{5,6},{6,7},{7,0},{8,9},{9,10},{10,1... | collective-permute-start | bytes 884744 | tf_op jit(solution)/shard_map/ppermute | solution.py:265
  36.7 9.1 %copy-start.11 = (bf16[48,3072]{1,0:T(8,128)(2,1)}, bf16[48,3072]{1,0:T(8,128)(2,1)S(1)}, u32[]{:S(2)}) copy-start(bf16[48,3072]{1,0:T(8,128)(2,1)S(1)} %collective-permute-done.12.refs_10_) | copy-start | bytes 884740
  36.7 11.3 %collective-permute-start.13 = (bf16[48,3072]{1,0:T(8,128)(2,1)S(1)}, bf16[48,3072]{1,0:T(8,128)(2,1)S(1)}, u32[]{:S(2)}, u32[]{:S(2)}) collective-permute-start(bf16[48,3072]{1,0:T(8,128)(2,1)S(1)} %collective-permute-done.12.refs_10_), channel_id=1, source_target_pairs={{0,7},{1,0},{2,1},{3,2},{4,3},{5,4},{6,5},{7,6},{8,15},{9,8},{10,9... | collective-permute-start | bytes 884744 | tf_op jit(solution)/shard_map/ppermute | solution.py:265
  37.9 4.1 %copy-start.14 = (bf16[48,3072]{1,0:T(8,128)(2,1)}, bf16[48,3072]{1,0:T(8,128)(2,1)S(1)}, u32[]{:S(2)}) copy-start(bf16[48,3072]{1,0:T(8,128)(2,1)S(1)} %collective-permute-done.3.refs_14_) | copy-start | bytes 884740
  41.7 0.8 copy-start.15
  44.7 0.8 copy-start.16
  45.0 0.7 copy-start.22
  45.1 0.8 copy-start.21
  48.0 0.8 copy-start.17
  48.9 18.8 %collective-permute-start.14 = (f32[64,768]{0,1:T(8,128)S(1)}, f32[64,768]{0,1:T(8,128)S(1)}, u32[]{:S(2)}, u32[]{:S(2)}) collective-permute-start(f32[64,768]{0,1:T(8,128)S(1)} %constant_dynamic-slice_fusion), channel_id=1, source_target_pairs={{0,8},{8,0},{1,9},{9,1},{2,10},{10,2},{3,11},{11,3},{4,12},{12,4},... | collective-permute-start | bytes 589832 | tf_op jit(solution)/shard_map/ppermute | solution.py:305
  109.7 4.5 %copy-start.1 = (bf16[8,48,512]{2,1,0:T(8,128)(2,1)}, bf16[8,48,512]{2,1,0:T(8,128)(2,1)S(1)}, u32[]{:S(2)}) copy-start(bf16[8,48,512]{2,1,0:T(8,128)(2,1)S(1)} %all_to_all.11.refs_2_) | copy-start | bytes 1179652
  109.7 4.4 %collective-permute-start.15 = (bf16[8,48,512]{2,1,0:T(8,128)(2,1)S(1)}, bf16[8,48,512]{2,1,0:T(8,128)(2,1)S(1)}, u32[]{:S(2)}, u32[]{:S(2)}) collective-permute-start(bf16[8,48,512]{2,1,0:T(8,128)(2,1)S(1)} %all_to_all.11.refs_2_), channel_id=1, source_target_pairs={{0,8},{8,0},{1,9},{9,1},{2,10},{10,2},{3,11},{11,3},{4,12},{12,4},... | collective-permute-start | bytes 1179656 | tf_op jit(solution)/shard_map/ppermute | solution.py:319
  112.8 1.4 copy-start.19
  112.8 1.4 collective-permute-start.16
  114.2 0.6 copy-start.23
  114.2 0.8 copy-start.18
